TPU v7x, 32 devices: a whole 2x2x4 slice. The times are simulated.
32 devices in a mesh: gx: 2 (over y), gy: 8 (over z, core), gz: 2 (over x).
Axes of the slice: x: 2, y: 2, z: 4, core: 2. Of those that a mesh axis runs over, the one named last changes fastest.
Arguments:
- starting_kelvin: float32 [16, 32, 2048], P(None, 'gx', ('gy', 'gz')), may hold values from -6 to 6
- substance_label: int32 [16, 32, 2048], P(None, 'gx', ('gy', 'gz')), may hold values from 0 to 3
- voxel_source_patch: int32 [16, 32, 2048], P(None, 'gx', ('gy', 'gz')), may hold values from 0 to 15
- substance_traits: float32 [4, 4], replicated, may hold values from 0.5 to 2
- patch_source_intensity: float32 [16], replicated, may hold values from 0 to 8
Outputs:
- warmed_result: float32 [16, 32, 2048], P(None, 'gx', ('gy', 'gz'))
- solution: float32 [3, 16, 32, 2048], P(None, 'gz', 'gx', 'gy')
- residual: float32 [3, 16, 32, 2048], P(None, 'gz', 'gx', 'gy')
All inputs are finite; a program needn't handle non-finite values.
Results may differ from a plain program's by a relative error of at most 0.0029.
Values sent between devices are 32-bit elements; how exact they have to be, the bound alone decides.
No kernel may reach another device: no remote copies, remote signals or barrier semaphores. Data moves between devices by JAX's collectives and lax.ppermute only.
A program may use at most 64 MiB of HBM per device.

v0:
```python
import jax
import jax.numpy as jnp
from jax import lax
from jax.sharding import PartitionSpec as P

ITERS = 3


time_step = 0.03
anchor_scale = 0.5
strain_gain = 2.0


def padded(value, sides, width):
    for axis, dim in sides:
        devices, length = (lax.axis_size(axis), value.shape[dim])
        up = [(i, (i + 1) % devices) for i in range(devices - 1)]
        down = [(j, i) for i, j in up]
        last = lax.slice_in_dim(value, length - width, length, axis=dim)
        initial = lax.slice_in_dim(value, 0, width, axis=dim)
        before = lax.ppermute(last, axis, up)
        after = lax.ppermute(initial, axis, down)
        value = jnp.concatenate([before, value, after], axis=dim)
    return value


def lookup(identity, table, count):
    summed = jnp.zeros(identity.shape, jnp.float32)
    for number in range(count):
        summed = summed + jnp.where(identity == number, table[number], jnp.float32(0.0))
    return summed


def conduct(own, other):
    return 2.0 * own * other / jnp.maximum(own + other, 0.25)


def heat_step(padded_temp, padded_cond, power, inverse_cap):
    centre = padded_temp[:, 1:-1, 1:-1]
    own = padded_cond[:, 1:-1, 1:-1]
    layers, rows, columns = centre.shape
    heat_flux = jnp.zeros_like(centre)
    for row_offset, column_offset in ((0, 1), (2, 1), (1, 0), (1, 2)):
        neighbour = padded_temp[
            :, row_offset : row_offset + rows, column_offset : column_offset + columns
        ]
        other = padded_cond[
            :, row_offset : row_offset + rows, column_offset : column_offset + columns
        ]
        heat_flux = heat_flux + conduct(own, other) * (neighbour - centre)
    vertical_temp = jnp.pad(centre, ((1, 1), (0, 0), (0, 0)))
    vertical_cond = jnp.pad(own, ((1, 1), (0, 0), (0, 0)))
    for layer_offset in (0, 2):
        other = vertical_cond[layer_offset : layer_offset + layers]
        neighbour = vertical_temp[layer_offset : layer_offset + layers]
        heat_flux = heat_flux + conduct(own, other) * (neighbour - centre)
    return centre + time_step * inverse_cap * (heat_flux + power)


def neighbour_offsets():
    listed = []
    for along_z in (-1, 0, 1):
        for along_x in (-1, 0, 1):
            for along_y in (-1, 0, 1):
                if along_z != 0 or along_x != 0 or along_y != 0:
                    listed.append((along_z, along_x, along_y))
    return listed


def apply_operator(field, padded_field, modulus, padded_modulus):
    layers, rows, columns = modulus.shape
    parts = [
        anchor_scale * modulus * field[0],
        anchor_scale * modulus * field[1],
        anchor_scale * modulus * field[2],
    ]
    for along_z, along_x, along_y in neighbour_offsets():
        length_sq = along_z * along_z + along_x * along_x + along_y * along_y
        window = (
            slice(1 + along_z, 1 + along_z + layers),
            slice(1 + along_x, 1 + along_x + rows),
            slice(1 + along_y, 1 + along_y + columns),
        )
        weight = 0.5 / length_sq * (modulus + padded_modulus[window])
        change = [field[index_c] - padded_field[index_c][window] for index_c in range(3)]
        projected = (along_z * change[0] + along_x * change[1] + along_y * change[2]) / length_sq
        for index_c, direction_part in enumerate((along_z, along_x, along_y)):
            parts[index_c] = parts[index_c] + weight * (
                0.5 * change[index_c] + direction_part * projected
            )
    return jnp.stack(parts)


def thermal_load(modulus, padded_modulus, strain, padded_strain):
    layers, rows, columns = modulus.shape
    parts = [jnp.zeros_like(modulus), jnp.zeros_like(modulus), jnp.zeros_like(modulus)]
    for along_z, along_x, along_y in neighbour_offsets():
        length_sq = along_z * along_z + along_x * along_x + along_y * along_y
        window = (
            slice(1 + along_z, 1 + along_z + layers),
            slice(1 + along_x, 1 + along_x + rows),
            slice(1 + along_y, 1 + along_y + columns),
        )
        weight = 0.5 / length_sq * (modulus + padded_modulus[window])
        pushing = weight * (0.5 * (strain + padded_strain[window]))
        for index_c, direction_part in enumerate((along_z, along_x, along_y)):
            if direction_part != 0:
                parts[index_c] = parts[index_c] - strain_gain * direction_part * pushing
    return jnp.stack(parts)


def two_products(residual, image):
    return lax.psum((jnp.sum(residual * residual), jnp.sum(residual * image)), ("gx", "gy", "gz"))


def per_device(
    starting_kelvin, substance_label, voxel_source_patch, substance_traits, patch_source_intensity
):
    count = substance_traits.shape[1]
    diffusive_coefficient = lookup(substance_label, substance_traits[0], count)
    inverse_cap = 1.0 / lookup(substance_label, substance_traits[1], count)
    power = lookup(voxel_source_patch, patch_source_intensity, patch_source_intensity.shape[0])
    padded_array = padded(
        jnp.stack([starting_kelvin, diffusive_coefficient]), (("gx", 2), (("gy", "gz"), 3)), 1
    )
    padded_cond = padded_array[1]
    warmed_result = heat_step(padded_array[0], padded_cond, power, inverse_cap)
    number = 0
    extended = padded(warmed_result, (("gx", 1), (("gy", "gz"), 2)), 1)
    warmed_result = heat_step(extended, padded_cond, power, inverse_cap)
    modulus = lookup(substance_label, substance_traits[2], count)
    strain = lookup(substance_label, substance_traits[3], count) * warmed_result
    fields = jnp.stack([modulus, strain])
    vertical_cycle = ((0, 0), (1, 1), (0, 0), (0, 0))
    padded_fields = jnp.pad(padded(fields, (("gx", 2), (("gy", "gz"), 3)), 1), vertical_cycle)

    def extend(field):
        return jnp.pad(padded(field, (("gx", 2), (("gy", "gz"), 3)), 1), vertical_cycle)

    modulus = fields[0]
    padded_modulus = padded_fields[0]
    load = thermal_load(modulus, padded_modulus, fields[1], padded_fields[1])

    def operate(field):
        return apply_operator(field, extend(field), modulus, padded_modulus)

    solution = jnp.zeros_like(load)
    residual = load
    image = operate(residual)
    norm_now, product = two_products(residual, image)
    alpha = norm_now / product
    direction, along_image = (residual, image)
    for number in range(ITERS):
        solution = solution + alpha * direction
        residual = residual - alpha * along_image
        if number + 1 < ITERS:
            image = operate(residual)
            norm_next, product = two_products(residual, image)
            ratio = norm_next / norm_now
            alpha = norm_next / (product - ratio * norm_next / alpha)
            direction = residual + ratio * direction
            along_image = image + ratio * along_image
            norm_now = norm_next
    joined = lax.all_to_all(
        jnp.concatenate([solution, residual]), "gz", split_axis=1, concat_axis=3, tiled=True
    )
    solution = joined[:3]
    residual = joined[3:]
    return (warmed_result, solution, residual)


def solution(mesh):
    in_specs = (
        P(None, "gx", ("gy", "gz")),
        P(None, "gx", ("gy", "gz")),
        P(None, "gx", ("gy", "gz")),
        P(),
        P(),
    )
    out_specs = (P(None, "gx", ("gy", "gz")), P(None, "gz", "gx", "gy"), P(None, "gz", "gx", "gy"))
    return jax.shard_map(
        per_device, mesh=mesh, in_specs=in_specs, out_specs=out_specs, check_vma=False
    )
```

profile of v0, /device:TPU:0, one launch (start us, length us, event | category | flops | bytes accessed | tf_op | source)
XLA Modules:
  0.0 370.7 jit_solution(7479689364601131842)
XLA Ops:
  9.6 4.9 %collective-permute-start = (f32[2,16,1,128]{3,1,2,0:T(8,128)S(1)}, f32[2,16,1,128]{3,1,2,0:T(8,128)S(1)}, u32[]{:S(2)}, u32[]{:S(2)}) collective-permute-start(f32[2,16,1,128]{3,1,2,0:T(8,128)S(1)} %get-tuple-element.112), channel_id=1, source_target_pairs={{0,16},{1,17},{2,18},{3,19},{4,20},{5,21},{6,22},{7,23},{8,24},{9,... | collective-permute-start | bytes 49160 | tf_op jit(solution)/shard_map/ppermute | solution.py:21
  15.9 4.2 %collective-permute-done.1 = f32[2,16,1,128]{3,1,2,0:T(8,128)S(1)} collective-permute-done((f32[2,16,1,128]{3,1,2,0:T(8,128)S(1)}, f32[2,16,1,128]{3,1,2,0:T(8,128)S(1)}, u32[]{:S(2)}, u32[]{:S(2)}) %collective-permute-start.1) | collective-permute-done | bytes 16416 | tf_op jit(solution)/shard_map/ppermute | solution.py:22
  25.8 8.3 %collective-permute-done.2 = f32[2,16,18,1]{3,1,2,0:T(8,128)S(1)} collective-permute-done((f32[2,16,18,1]{3,1,2,0:T(8,128)S(1)}, f32[2,16,18,1]{3,1,2,0:T(8,128)S(1)}, u32[]{:S(2)}, u32[]{:S(2)}) %collective-permute-start.2) | collective-permute-done | bytes 2336 | tf_op jit(solution)/shard_map/ppermute | solution.py:21
  35.3 13.0 %fusion.8 = f32[16,16,128]{2,0,1:T(8,128)S(1)} fusion(f32[16,16,128]{2,0,1:T(8,128)S(1)} %slice.2049, f32[16,18,130]{2,0,1:T(8,128)S(1)} %get-tuple-element.91, pred[16,16,128]{2,0,1:T(8,128)(4,1)S(1)} %get-tuple-element.74, f32[]{:T(128)} %bitcast.10, pred[16,16,128]{2,0,1:T(8,128)(4,1)S(1)} %get-tuple-element.73, f32[]{:T(128)} %bitcast.9, ...), kind=kLoop, calls=%fused_computation.73 | loop fusion | flops 3342336 | bytes 1835088 | tf_op jit(solution)/shard_map/add | solution.py:57
  55.6 4.8 %collective-permute-start.6 = (f32[16,18,1]{2,0,1:T(8,128)S(1)}, f32[16,18,1]{2,0,1:T(8,128)S(1)}, u32[]{:S(2)}, u32[]{:S(2)}) collective-permute-start(f32[16,18,1]{2,0,1:T(8,128)S(1)} %get-tuple-element.114), channel_id=1, source_target_pairs={{0,1},{1,2},{2,3},{3,4},{4,5},{5,6},{6,7},{7,8},{8,9},{9,10},{10,1... | collective-permute-start | bytes 3464 | tf_op jit(solution)/shard_map/ppermute | solution.py:21
  63.3 5.1 %collective-permute-done.7 = f32[16,18,1]{2,0,1:T(8,128)S(1)} collective-permute-done((f32[16,18,1]{2,0,1:T(8,128)S(1)}, f32[16,18,1]{2,0,1:T(8,128)S(1)}, u32[]{:S(2)}, u32[]{:S(2)}) %collective-permute-start.7) | collective-permute-done | bytes 1184 | tf_op jit(solution)/shard_map/ppermute | solution.py:22
  68.3 15.6 %add_multiply_fusion.6 = (f32[16,16,128]{2,0,1:T(8,128)S(1)}, f32[16,16,128]{2,0,1:T(8,128)S(1)}) fusion(pred[16,16,128]{2,0,1:T(8,128)(4,1)S(1)} %get-tuple-element.74, pred[16,16,128]{2,0,1:T(8,128)(4,1)S(1)} %get-tuple-element.73, pred[16,16,128]{2,0,1:T(8,128)(4,1)S(1)} %get-tuple-element.72, pred[16,16,128]{2,0,1:T(8,128)(4,1)S(1)} %get-tuple-element.71, ...), kind=kLoop, calls=%fused_computation.625 | loop fusion | flops 3866624 | bytes 1460576 | tf_op jit(solution)/shard_map/mul | solution.py:132
  94.1 5.2 %collective-permute-done.10 = f32[2,16,18,1]{3,1,2,0:T(8,128)S(1)} collective-permute-done((f32[2,16,18,1]{3,1,2,0:T(8,128)S(1)}, f32[2,16,18,1]{3,1,2,0:T(8,128)S(1)}, u32[]{:S(2)}, u32[]{:S(2)}) %collective-permute-start.10) | collective-permute-done | bytes 2336 | tf_op jit(solution)/shard_map/ppermute | solution.py:21
  99.3 4.7 %collective-permute-done.11 = f32[2,16,18,1]{3,1,2,0:T(8,128)S(1)} collective-permute-done((f32[2,16,18,1]{3,1,2,0:T(8,128)S(1)}, f32[2,16,18,1]{3,1,2,0:T(8,128)S(1)}, u32[]{:S(2)}, u32[]{:S(2)}) %collective-permute-start.11) | collective-permute-done | bytes 2336 | tf_op jit(solution)/shard_map/ppermute | solution.py:22
  118.4 4.2 %collective-permute-done.13 = f32[3,16,1,128]{3,1,2,0:T(8,128)S(1)} collective-permute-done((f32[3,16,1,128]{3,1,2,0:T(8,128)S(1)}, f32[3,16,1,128]{3,1,2,0:T(8,128)S(1)}, u32[]{:S(2)}, u32[]{:S(2)}) %collective-permute-start.13) | collective-permute-done | bytes 24608 | tf_op jit(solution)/shard_map/ppermute | solution.py:22
  123.3 6.3 %collective-permute-start.14 = (f32[3,16,18,1]{2,1,3,0:T(8,128)S(1)}, f32[3,16,18,1]{2,1,3,0:T(8,128)S(1)}, u32[]{:S(2)}, u32[]{:S(2)}) collective-permute-start(f32[3,16,18,1]{2,1,3,0:T(8,128)S(1)} %copy.174), channel_id=1, source_target_pairs={{0,1},{1,2},{2,3},{3,4},{4,5},{5,6},{6,7},{7,8},{8,9},{9,10},{10,1... | collective-permute-start | bytes 10376 | tf_op jit(solution)/shard_map/ppermute | solution.py:21
  137.0 5.2 %add_bitcast_fusion.7 = f32[1,16,16,128]{3,1,2,0:T(8,128)S(1)} fusion(f32[16,16,128]{2,0,1:T(8,128)S(1)} %fusion.52, f32[16,16,128]{2,0,1:T(8,128)S(1)} %fusion.93, f32[18,18,130]{2,0,1:T(8,128)S(1)} %get-tuple-element.85, f32[18,18,130]{2,0,1:T(8,128)S(1)} %get-tuple-element.84, f32[16,16,128]{2,0,1:T(8,128)S(1)} %fusion.31, ...), kind=kLoop, calls=%fused_computation.599 | loop fusion | flops 11862016 | bytes 14286864 | tf_op jit(solution)/shard_map/stack | solution.py:91
  142.2 5.2 %add_bitcast_fusion.6 = f32[1,16,16,128]{3,1,2,0:T(8,128)S(1)} fusion(f32[16,16,128]{2,0,1:T(8,128)S(1)} %fusion.31, f32[16,16,128]{2,0,1:T(8,128)S(1)} %fusion.93, f32[18,18,130]{2,0,1:T(8,128)S(1)} %get-tuple-element.85, f32[16,16,128]{2,0,1:T(8,128)S(1)} %fusion.52, f32[18,18,130]{2,0,1:T(8,128)S(1)} %get-tuple-element.84, ...), kind=kLoop, calls=%fused_computation.598 | loop fusion | flops 11862016 | bytes 14286864 | tf_op jit(solution)/shard_map/stack | solution.py:91
  147.4 5.2 %add_bitcast_fusion.8 = f32[1,16,16,128]{3,1,2,0:T(8,128)S(1)} fusion(f32[16,16,128]{2,0,1:T(8,128)S(1)} %fusion.93, f32[18,18,130]{2,0,1:T(8,128)S(1)} %get-tuple-element.85, f32[16,16,128]{2,0,1:T(8,128)S(1)} %fusion.52, f32[18,18,130]{2,0,1:T(8,128)S(1)} %get-tuple-element.84, f32[16,16,128]{2,0,1:T(8,128)S(1)} %fusion.31, ...), kind=kLoop, calls=%fused_computation.600 | loop fusion | flops 11862016 | bytes 14286864 | tf_op jit(solution)/shard_map/stack | solution.py:91
  153.3 40.6 %all-reduce.9 = (f32[]{:T(128)}, f32[]{:T(128)}) all-reduce(f32[]{:T(128)} %get-tuple-element.17, f32[]{:T(128)} %get-tuple-element.16), channel_id=1, replica_groups=mesh['gx'=2,'gy'=8,'gz'=2] {'gx','gy','gz'}, use_global_device_ids=true, to_apply=%region_1.2 | all-reduce | flops 2 | bytes 16 | tf_op jit(solution)/shard_map/psum | solution.py:113
  195.3 4.4 %collective-permute-start.16 = (f32[3,16,1,128]{3,1,2,0:T(8,128)S(1)}, f32[3,16,1,128]{3,1,2,0:T(8,128)S(1)}, u32[]{:S(2)}, u32[]{:S(2)}) collective-permute-start(f32[3,16,1,128]{3,1,2,0:T(8,128)S(1)} %get-tuple-element.102), channel_id=1, source_target_pairs={{0,16},{1,17},{2,18},{3,19},{4,20},{5,21},{6,22},{7,23},{8,24},{9,... | collective-permute-start | bytes 73736 | tf_op jit(solution)/shard_map/ppermute | solution.py:21
  201.2 4.2 %collective-permute-done.17 = f32[3,16,1,128]{3,1,2,0:T(8,128)S(1)} collective-permute-done((f32[3,16,1,128]{3,1,2,0:T(8,128)S(1)}, f32[3,16,1,128]{3,1,2,0:T(8,128)S(1)}, u32[]{:S(2)}, u32[]{:S(2)}) %collective-permute-start.17) | collective-permute-done | bytes 24608 | tf_op jit(solution)/shard_map/ppermute | solution.py:22
  215.3 5.4 %add_bitcast_fusion.5 = (f32[1,16,16,128]{3,1,2,0:T(8,128)S(1)}, f32[16,16,128]{2,0,1:T(8,128)S(1)}, f32[16,16,128]{2,0,1:T(8,128)S(1)}, f32[16,16,128]{2,0,1:T(...) fusion(f32[18,18,130]{2,0,1:T(8,128)S(1)} %get-tuple-element.82, ...), kind=kLoop, calls=%fused_computation.573 | loop fusion | flops 11862016 | bytes 17170448 | tf_op jit(solution)/shard_map/stack | solution.py:91
  229.7 39.7 %all-reduce.8 = (f32[]{:T(128)}, f32[]{:T(128)}) all-reduce(f32[]{:T(128)} %get-tuple-element.15, f32[]{:T(128)} %get-tuple-element.14), channel_id=1, replica_groups=mesh['gx'=2,'gy'=8,'gz'=2] {'gx','gy','gz'}, use_global_device_ids=true, to_apply=%region_5.6 | all-reduce | flops 2 | bytes 16 | tf_op jit(solution)/shard_map/psum | solution.py:113
  274.2 4.4 %collective-permute-start.20 = (f32[3,16,1,128]{3,1,2,0:T(8,128)S(1)}, f32[3,16,1,128]{3,1,2,0:T(8,128)S(1)}, u32[]{:S(2)}, u32[]{:S(2)}) collective-permute-start(f32[3,16,1,128]{3,1,2,0:T(8,128)S(1)} %get-tuple-element.100), channel_id=1, source_target_pairs={{0,16},{1,17},{2,18},{3,19},{4,20},{5,21},{6,22},{7,23},{8,24},{9,... | collective-permute-start | bytes 73736 | tf_op jit(solution)/shard_map/ppermute | solution.py:21
  280.1 4.2 %collective-permute-done.21 = f32[3,16,1,128]{3,1,2,0:T(8,128)S(1)} collective-permute-done((f32[3,16,1,128]{3,1,2,0:T(8,128)S(1)}, f32[3,16,1,128]{3,1,2,0:T(8,128)S(1)}, u32[]{:S(2)}, u32[]{:S(2)}) %collective-permute-start.21) | collective-permute-done | bytes 24608 | tf_op jit(solution)/shard_map/ppermute | solution.py:22
  294.1 5.4 %add_bitcast_fusion.2 = (f32[1,16,16,128]{3,1,2,0:T(8,128)S(1)}, f32[16,16,128]{2,0,1:T(8,128)S(1)}, f32[16,16,128]{2,0,1:T(8,128)S(1)}, f32[16,16,128]{2,0,1:T(...) fusion(f32[18,18,130]{2,0,1:T(8,128)S(1)} %get-tuple-element.79, ...), kind=kLoop, calls=%fused_computation.546 | loop fusion | flops 11862016 | bytes 17170448 | tf_op jit(solution)/shard_map/stack | solution.py:91
  308.6 39.8 %all-reduce.7 = (f32[]{:T(128)}, f32[]{:T(128)}) all-reduce(f32[]{:T(128)} %get-tuple-element.13, f32[]{:T(128)} %get-tuple-element.12), channel_id=1, replica_groups=mesh['gx'=2,'gy'=8,'gz'=2] {'gx','gy','gz'}, use_global_device_ids=true, to_apply=%region_9.10 | all-reduce | flops 2 | bytes 16 | tf_op jit(solution)/shard_map/psum | solution.py:113
  358.2 9.7 %all-to-all-done = f32[6,16,16,128]{3,2,0,1:T(8,128)S(1)} async-done(((f32[6,16,16,128]{3,2,0,1:T(8,128)}), f32[6,16,16,128]{3,2,0,1:T(8,128)S(1)}, u32[]{:S(2)}, u32[]{:S(2)}) %all-to-all-start) | async-done | bytes 786464 | tf_op jit(solution)/shard_map/all_to_all | solution.py:164
  (108 shorter events, 109.9 us)
Async XLA Ops:
  9.6 6.3 %collective-permute-start = (f32[2,16,1,128]{3,1,2,0:T(8,128)S(1)}, f32[2,16,1,128]{3,1,2,0:T(8,128)S(1)}, u32[]{:S(2)}, u32[]{:S(2)}) collective-permute-start(f32[2,16,1,128]{3,1,2,0:T(8,128)S(1)} %get-tuple-element.112), channel_id=1, source_target_pairs={{0,16},{1,17},{2,18},{3,19},{4,20},{5,21},{6,22},{7,23},{8,24},{9,... | collective-permute-start | bytes 49160 | tf_op jit(solution)/shard_map/ppermute | solution.py:21
  14.5 5.6 %collective-permute-start.1 = (f32[2,16,1,128]{3,1,2,0:T(8,128)S(1)}, f32[2,16,1,128]{3,1,2,0:T(8,128)S(1)}, u32[]{:S(2)}, u32[]{:S(2)}) collective-permute-start(f32[2,16,1,128]{3,1,2,0:T(8,128)S(1)} %get-tuple-element.113), channel_id=1, source_target_pairs={{16,0},{17,1},{18,2},{19,3},{20,4},{21,5},{22,6},{23,7},{24,8},{25... | collective-permute-start | bytes 49160 | tf_op jit(solution)/shard_map/ppermute | solution.py:22
  20.3 13.8 %collective-permute-start.2 = (f32[2,16,18,1]{3,1,2,0:T(8,128)S(1)}, f32[2,16,18,1]{3,1,2,0:T(8,128)S(1)}, u32[]{:S(2)}, u32[]{:S(2)}) collective-permute-start(f32[2,16,18,1]{3,1,2,0:T(8,128)S(1)} %get-tuple-element.108), channel_id=1, source_target_pairs={{0,1},{1,2},{2,3},{3,4},{4,5},{5,6},{6,7},{7,8},{8,9},{9,10},{10,1... | collective-permute-start | bytes 6920 | tf_op jit(solution)/shard_map/ppermute | solution.py:21
  23.7 11.0 %collective-permute-start.3 = (f32[2,16,18,1]{3,1,2,0:T(8,128)S(1)}, f32[2,16,18,1]{3,1,2,0:T(8,128)S(1)}, u32[]{:S(2)}, u32[]{:S(2)}) collective-permute-start(f32[2,16,18,1]{3,1,2,0:T(8,128)S(1)} %get-tuple-element.109), channel_id=1, source_target_pairs={{1,0},{2,1},{3,2},{4,3},{5,4},{6,5},{7,6},{8,7},{9,8},{10,9},{11,1... | collective-permute-start | bytes 6920 | tf_op jit(solution)/shard_map/ppermute | solution.py:22
  49.9 5.5 %collective-permute-start.5 = (f32[16,1,128]{2,0,1:T(8,128)S(1)}, f32[16,1,128]{2,0,1:T(8,128)S(1)}, u32[]{:S(2)}, u32[]{:S(2)}) collective-permute-start(f32[16,1,128]{2,0,1:T(8,128)S(1)} %get-tuple-element.117), channel_id=1, source_target_pairs={{16,0},{17,1},{18,2},{19,3},{20,4},{21,5},{22,6},{23,7},{24,8},{25... | collective-permute-start | bytes 24584 | tf_op jit(solution)/shard_map/ppermute | solution.py:22
  55.6 7.7 %collective-permute-start.6 = (f32[16,18,1]{2,0,1:T(8,128)S(1)}, f32[16,18,1]{2,0,1:T(8,128)S(1)}, u32[]{:S(2)}, u32[]{:S(2)}) collective-permute-start(f32[16,18,1]{2,0,1:T(8,128)S(1)} %get-tuple-element.114), channel_id=1, source_target_pairs={{0,1},{1,2},{2,3},{3,4},{4,5},{5,6},{6,7},{7,8},{8,9},{9,10},{10,1... | collective-permute-start | bytes 3464 | tf_op jit(solution)/shard_map/ppermute | solution.py:21
  60.4 7.9 %collective-permute-start.7 = (f32[16,18,1]{2,0,1:T(8,128)S(1)}, f32[16,18,1]{2,0,1:T(8,128)S(1)}, u32[]{:S(2)}, u32[]{:S(2)}) collective-permute-start(f32[16,18,1]{2,0,1:T(8,128)S(1)} %get-tuple-element.115), channel_id=1, source_target_pairs={{1,0},{2,1},{3,2},{4,3},{5,4},{6,5},{7,6},{8,7},{9,8},{10,9},{11,1... | collective-permute-start | bytes 3464 | tf_op jit(solution)/shard_map/ppermute | solution.py:22
  83.9 3.1 collective-permute-start.8
  85.5 5.6 %collective-permute-start.9 = (f32[2,16,1,128]{3,1,2,0:T(8,128)S(1)}, f32[2,16,1,128]{3,1,2,0:T(8,128)S(1)}, u32[]{:S(2)}, u32[]{:S(2)}) collective-permute-start(f32[2,16,1,128]{3,1,2,0:T(8,128)S(1)} %get-tuple-element.111), channel_id=1, source_target_pairs={{16,0},{17,1},{18,2},{19,3},{20,4},{21,5},{22,6},{23,7},{24,8},{25... | collective-permute-start | bytes 49160 | tf_op jit(solution)/shard_map/ppermute | solution.py:22
  91.4 7.9 %collective-permute-start.10 = (f32[2,16,18,1]{3,1,2,0:T(8,128)S(1)}, f32[2,16,18,1]{3,1,2,0:T(8,128)S(1)}, u32[]{:S(2)}, u32[]{:S(2)}) collective-permute-start(f32[2,16,18,1]{3,1,2,0:T(8,128)S(1)} %get-tuple-element.106), channel_id=1, source_target_pairs={{0,1},{1,2},{2,3},{3,4},{4,5},{5,6},{6,7},{7,8},{8,9},{9,10},{10,1... | collective-permute-start | bytes 6920 | tf_op jit(solution)/shard_map/ppermute | solution.py:21
  92.8 11.1 %collective-permute-start.11 = (f32[2,16,18,1]{3,1,2,0:T(8,128)S(1)}, f32[2,16,18,1]{3,1,2,0:T(8,128)S(1)}, u32[]{:S(2)}, u32[]{:S(2)}) collective-permute-start(f32[2,16,18,1]{3,1,2,0:T(8,128)S(1)} %get-tuple-element.107), channel_id=1, source_target_pairs={{1,0},{2,1},{3,2},{4,3},{5,4},{6,5},{7,6},{8,7},{9,8},{10,9},{11,1... | collective-permute-start | bytes 6920 | tf_op jit(solution)/shard_map/ppermute | solution.py:22
  114.7 3.7 %collective-permute-start.12 = (f32[3,16,1,128]{3,1,2,0:T(8,128)S(1)}, f32[3,16,1,128]{3,1,2,0:T(8,128)S(1)}, u32[]{:S(2)}, u32[]{:S(2)}) collective-permute-start(f32[3,16,1,128]{3,1,2,0:T(8,128)S(1)} %get-tuple-element.104), channel_id=1, source_target_pairs={{0,16},{1,17},{2,18},{3,19},{4,20},{5,21},{6,22},{7,23},{8,24},{9,... | collective-permute-start | bytes 73736 | tf_op jit(solution)/shard_map/ppermute | solution.py:21
  116.9 5.7 %collective-permute-start.13 = (f32[3,16,1,128]{3,1,2,0:T(8,128)S(1)}, f32[3,16,1,128]{3,1,2,0:T(8,128)S(1)}, u32[]{:S(2)}, u32[]{:S(2)}) collective-permute-start(f32[3,16,1,128]{3,1,2,0:T(8,128)S(1)} %get-tuple-element.105), channel_id=1, source_target_pairs={{16,0},{17,1},{18,2},{19,3},{20,4},{21,5},{22,6},{23,7},{24,8},{25... | collective-permute-start | bytes 73736 | tf_op jit(solution)/shard_map/ppermute | solution.py:22
  123.3 8.2 %collective-permute-start.14 = (f32[3,16,18,1]{2,1,3,0:T(8,128)S(1)}, f32[3,16,18,1]{2,1,3,0:T(8,128)S(1)}, u32[]{:S(2)}, u32[]{:S(2)}) collective-permute-start(f32[3,16,18,1]{2,1,3,0:T(8,128)S(1)} %copy.174), channel_id=1, source_target_pairs={{0,1},{1,2},{2,3},{3,4},{4,5},{5,6},{6,7},{7,8},{8,9},{9,10},{10,1... | collective-permute-start | bytes 10376 | tf_op jit(solution)/shard_map/ppermute | solution.py:21
  130.0 5.8 %collective-permute-start.15 = (f32[3,16,18,1]{2,1,3,0:T(8,128)S(1)}, f32[3,16,18,1]{2,1,3,0:T(8,128)S(1)}, u32[]{:S(2)}, u32[]{:S(2)}) collective-permute-start(f32[3,16,18,1]{2,1,3,0:T(8,128)S(1)} %copy.175), channel_id=1, source_target_pairs={{1,0},{2,1},{3,2},{4,3},{5,4},{6,5},{7,6},{8,7},{9,8},{10,9},{11,1... | collective-permute-start | bytes 10376 | tf_op jit(solution)/shard_map/ppermute | solution.py:22
  195.3 5.9 %collective-permute-start.16 = (f32[3,16,1,128]{3,1,2,0:T(8,128)S(1)}, f32[3,16,1,128]{3,1,2,0:T(8,128)S(1)}, u32[]{:S(2)}, u32[]{:S(2)}) collective-permute-start(f32[3,16,1,128]{3,1,2,0:T(8,128)S(1)} %get-tuple-element.102), channel_id=1, source_target_pairs={{0,16},{1,17},{2,18},{3,19},{4,20},{5,21},{6,22},{7,23},{8,24},{9,... | collective-permute-start | bytes 73736 | tf_op jit(solution)/shard_map/ppermute | solution.py:21
  199.7 5.7 %collective-permute-start.17 = (f32[3,16,1,128]{3,1,2,0:T(8,128)S(1)}, f32[3,16,1,128]{3,1,2,0:T(8,128)S(1)}, u32[]{:S(2)}, u32[]{:S(2)}) collective-permute-start(f32[3,16,1,128]{3,1,2,0:T(8,128)S(1)} %get-tuple-element.103), channel_id=1, source_target_pairs={{16,0},{17,1},{18,2},{19,3},{20,4},{21,5},{22,6},{23,7},{24,8},{25... | collective-permute-start | bytes 73736 | tf_op jit(solution)/shard_map/ppermute | solution.py:22
  206.0 3.9 %collective-permute-start.18 = (f32[3,16,18,1]{2,1,3,0:T(8,128)S(1)}, f32[3,16,18,1]{2,1,3,0:T(8,128)S(1)}, u32[]{:S(2)}, u32[]{:S(2)}) collective-permute-start(f32[3,16,18,1]{2,1,3,0:T(8,128)S(1)} %copy.190), channel_id=1, source_target_pairs={{0,1},{1,2},{2,3},{3,4},{4,5},{5,6},{6,7},{7,8},{8,9},{9,10},{10,1... | collective-permute-start | bytes 10376 | tf_op jit(solution)/shard_map/ppermute | solution.py:21
  208.5 5.7 %collective-permute-start.19 = (f32[3,16,18,1]{2,1,3,0:T(8,128)S(1)}, f32[3,16,18,1]{2,1,3,0:T(8,128)S(1)}, u32[]{:S(2)}, u32[]{:S(2)}) collective-permute-start(f32[3,16,18,1]{2,1,3,0:T(8,128)S(1)} %copy.191), channel_id=1, source_target_pairs={{1,0},{2,1},{3,2},{4,3},{5,4},{6,5},{7,6},{8,7},{9,8},{10,9},{11,1... | collective-permute-start | bytes 10376 | tf_op jit(solution)/shard_map/ppermute | solution.py:22
  274.2 5.9 %collective-permute-start.20 = (f32[3,16,1,128]{3,1,2,0:T(8,128)S(1)}, f32[3,16,1,128]{3,1,2,0:T(8,128)S(1)}, u32[]{:S(2)}, u32[]{:S(2)}) collective-permute-start(f32[3,16,1,128]{3,1,2,0:T(8,128)S(1)} %get-tuple-element.100), channel_id=1, source_target_pairs={{0,16},{1,17},{2,18},{3,19},{4,20},{5,21},{6,22},{7,23},{8,24},{9,... | collective-permute-start | bytes 73736 | tf_op jit(solution)/shard_map/ppermute | solution.py:21
  278.6 5.7 %collective-permute-start.21 = (f32[3,16,1,128]{3,1,2,0:T(8,128)S(1)}, f32[3,16,1,128]{3,1,2,0:T(8,128)S(1)}, u32[]{:S(2)}, u32[]{:S(2)}) collective-permute-start(f32[3,16,1,128]{3,1,2,0:T(8,128)S(1)} %get-tuple-element.101), channel_id=1, source_target_pairs={{16,0},{17,1},{18,2},{19,3},{20,4},{21,5},{22,6},{23,7},{24,8},{25... | collective-permute-start | bytes 73736 | tf_op jit(solution)/shard_map/ppermute | solution.py:22
  285.0 3.9 %collective-permute-start.22 = (f32[3,16,18,1]{2,1,3,0:T(8,128)S(1)}, f32[3,16,18,1]{2,1,3,0:T(8,128)S(1)}, u32[]{:S(2)}, u32[]{:S(2)}) collective-permute-start(f32[3,16,18,1]{2,1,3,0:T(8,128)S(1)} %copy.192), channel_id=1, source_target_pairs={{0,1},{1,2},{2,3},{3,4},{4,5},{5,6},{6,7},{7,8},{8,9},{9,10},{10,1... | collective-permute-start | bytes 10376 | tf_op jit(solution)/shard_map/ppermute | solution.py:21
  287.3 5.7 %collective-permute-start.23 = (f32[3,16,18,1]{2,1,3,0:T(8,128)S(1)}, f32[3,16,18,1]{2,1,3,0:T(8,128)S(1)}, u32[]{:S(2)}, u32[]{:S(2)}) collective-permute-start(f32[3,16,18,1]{2,1,3,0:T(8,128)S(1)} %copy.193), channel_id=1, source_target_pairs={{1,0},{2,1},{3,2},{4,3},{5,4},{6,5},{7,6},{8,7},{9,8},{10,9},{11,1... | collective-permute-start | bytes 10376 | tf_op jit(solution)/shard_map/ppermute | solution.py:22
  353.9 14.0 %all-to-all-start = ((f32[6,16,16,128]{3,2,0,1:T(8,128)}), f32[6,16,16,128]{3,2,0,1:T(8,128)S(1)}, u32[]{:S(2)}, u32[]{:S(2)}) async-start(f32[6,16,16,128]{3,2,0,1:T(8,128)} %copy.186), calls=%async_computation | async-start | bytes 1572864 | tf_op jit(solution)/shard_map/all_to_all | solution.py:164
  (3 other events, 31.5 us)
where the time goes:
time: 373 us; the launch traced here: 371 us
  blocking collectives  120 us (32%)
  other arithmetic  94.1 us (25%)
  waiting for transfers between devices  72.8 us (20%)
  starting transfers between devices  58.9 us (16%)
  local copies, waits for them, and re-layouts  13.6 us (4%)
  between operations  11.3 us (3%)
    psum x3, blocking collectives, two_products(): lax.psum((jnp.sum(residual * residual), jnp.sum(residual * image)), ('gx'...  120 us
    ppermute x12, waiting for transfers between devices, padded(): after = lax.ppermute(initial, axis, down)  47.1 us
    another operation x9, other arithmetic, apply_operator(): return jnp.stack(parts)  42.9 us
    ppermute x12, starting transfers between devices, padded(): before = lax.ppermute(last, axis, up)  39.2 us
    ppermute x12, starting transfers between devices, padded(): after = lax.ppermute(initial, axis, down)  16.1 us
    ppermute x12, waiting for transfers between devices, padded(): before = lax.ppermute(last, axis, up)  16 us
    mul x1, other arithmetic, per_device(): strain = lookup(substance_label, substance_traits[3], count) * warmed_result  15.6 us
    add x1, other arithmetic, heat_step(): return centre + time_step * inverse_cap * (heat_flux + power)  13 us
  transfers between devices with their start and end apart: 25, of which 21 were waited for; matrix products, arithmetic and copies ran while one was open for 1% of the time, Pallas kernels for 0%

commit v1 on v0

--- a/solution.py
+++ b/solution.py
@@ -1,14 +1,589 @@
+import functools
+
 import jax
 import jax.numpy as jnp
 from jax import lax
+from jax.experimental import pallas as pl
+from jax.experimental.pallas import tpu as pltpu
 from jax.sharding import PartitionSpec as P
 
 ITERS = 3
-
+HEAT_STEPS = 2
+HALO = 8
+LANES = 128
+PAD = 8
+AXES = ("gx", "gy", "gz")
 
 time_step = 0.03
 anchor_scale = 0.5
 strain_gain = 2.0
+CENTRE = 55.0 / 9.0
+
+f32 = jnp.float32
+
+
+def half_roll(x):
+    return pltpu.roll(x, LANES // 2, 1)
+
+
+def lane_of(shape):
+    return lax.broadcasted_iota(jnp.int32, shape, 1)
+
+
+def pack_rows_kernel(where_ref, temp, label, patch, out):
+    layers, rows, _ = temp.shape
+    half = layers // 2
+    theirs = 1 - where_ref[2]
+    lane = lane_of((rows, LANES))
+    in_half = (lane // (LANES // 2)) == theirs
+    base = LANES // 2 - HALO * theirs
+    for a, ref in enumerate((temp, label, patch)):
+        for l in range(half):
+            low = ref[l].astype(f32)
+            high = ref[l + half].astype(f32)
+            out[a, l] = jnp.where(in_half, low, half_roll(high))
+        near = jnp.zeros((rows, LANES), f32)
+        for l in range(layers):
+            moved = pltpu.roll(ref[l].astype(f32), (HALO * l - base) % LANES, 1)
+            near = jnp.where((lane // HALO) == l, moved, near)
+        out[a, half] = near
+
+
+def pack_far_kernel(where_ref, temp, label, patch, got, out):
+    layers, rows, _ = temp.shape
+    half = layers // 2
+    gx = where_ref[0]
+    pos = where_ref[2]
+    lane = lane_of((rows, LANES))
+    base = (LANES - HALO) * pos
+    own = pl.multiple_of(gx * rows, rows)
+    other = pl.multiple_of((1 - gx) * rows, rows)
+    for a, ref in enumerate((temp, label, patch)):
+        mine = jnp.zeros((rows, LANES), f32)
+        theirs = jnp.zeros((rows, LANES), f32)
+        for l in range(layers):
+            here = (lane // HALO) == l
+            moved = pltpu.roll(ref[l].astype(f32), (HALO * l - base) % LANES, 1)
+            mine = jnp.where(here, moved, mine)
+            extra = 0 if l < half else LANES // 2
+            moved = pltpu.roll(got[a, l % half], (HALO * l - base + extra) % LANES, 1)
+            theirs = jnp.where(here, moved, theirs)
+        out[a, pl.ds(own, rows), :] = mine
+        out[a, pl.ds(other, rows), :] = theirs
+
+
+def picks(ref, index, l, row):
+    def at(dz, dx):
+        if index is None:
+            return ref[l + 1 + dz, PAD + row + dx : PAD + row + dx + 8, :]
+        return ref[index[0], index[1], l + 1 + dz, PAD + row + dx : PAD + row + dx + 8, :]
+
+    out = {}
+    for dx in (-1, 0, 1):
+        up, mid, down = at(1, dx), at(0, dx), at(-1, dx)
+        out["F", dx] = mid
+        out["G", dx] = up + down
+        out["H", dx] = up - down
+    res = {}
+    for k in "FGH":
+        res[k] = out[k, 0]
+        res["E" + k] = out[k, 1] + out[k, -1]
+        res["D" + k] = out[k, 1] - out[k, -1]
+    return res
+
+
+def along_lanes(base, even, odd):
+    total = base
+    if odd is None:
+        return total + pltpu.roll(even, LANES - 1, 1) + pltpu.roll(even, 1, 1)
+    if even is None:
+        return total + pltpu.roll(odd, LANES - 1, 1) - pltpu.roll(odd, 1, 1)
+    return total + pltpu.roll(even + odd, LANES - 1, 1) + pltpu.roll(even - odd, 1, 1)
+
+
+S9 = 5.0 / 36.0
+S18 = 1.0 / 18.0
+S6 = 1.0 / 6.0
+
+
+def full_stencil(z, x, y):
+    base0 = 0.25 * (z["EF"] + z["EG"]) + 0.75 * z["G"] + 0.125 * x["DH"]
+    even0 = 0.25 * (z["F"] + z["G"]) + 0.125 * z["EF"] + S9 * z["EG"] + S18 * x["DH"]
+    odd0 = 0.125 * y["H"] + S18 * y["EH"]
+    base1 = 0.75 * x["EF"] + 0.25 * (x["G"] + x["EG"]) + 0.125 * z["DH"]
+    even1 = 0.25 * (x["F"] + x["EF"]) + 0.125 * x["G"] + S9 * x["EG"] + S18 * z["DH"]
+    odd1 = 0.125 * y["DF"] + S18 * y["DG"]
+    base2 = 0.25 * (y["EF"] + y["G"]) + 0.125 * y["EG"]
+    even2 = 0.75 * y["F"] + 0.25 * (y["EF"] + y["G"]) + S9 * y["EG"]
+    odd2 = 0.125 * (x["DF"] + z["H"]) + S18 * (x["DG"] + z["EH"])
+    return (
+        along_lanes(base0, even0, odd0),
+        along_lanes(base1, even1, odd1),
+        along_lanes(base2, even2, odd2),
+    )
+
+
+def matrix_stencil(m):
+    zz = along_lanes(
+        0.25 * (m["EF"] + m["EG"]) + 0.75 * m["G"],
+        0.25 * (m["F"] + m["G"]) + 0.125 * m["EF"] + S9 * m["EG"],
+        None,
+    )
+    xx = along_lanes(
+        0.75 * m["EF"] + 0.25 * (m["G"] + m["EG"]),
+        0.25 * (m["F"] + m["EF"]) + 0.125 * m["G"] + S9 * m["EG"],
+        None,
+    )
+    yy = along_lanes(
+        0.25 * (m["EF"] + m["G"]) + 0.125 * m["EG"],
+        0.75 * m["F"] + 0.25 * (m["EF"] + m["G"]) + S9 * m["EG"],
+        None,
+    )
+    zx = along_lanes(0.125 * m["DH"], S18 * m["DH"], None)
+    odd_zy = 0.125 * m["H"] + S18 * m["EH"]
+    odd_xy = 0.125 * m["DF"] + S18 * m["DG"]
+    zy = pltpu.roll(odd_zy, LANES - 1, 1) - pltpu.roll(odd_zy, 1, 1)
+    xy = pltpu.roll(odd_xy, LANES - 1, 1) - pltpu.roll(odd_xy, 1, 1)
+    return zz, xx, yy, zx, zy, xy
+
+
+def gradient_stencil(f):
+    gz = along_lanes(0.5 * f["H"] + 0.25 * f["EH"], 0.25 * f["H"] + S6 * f["EH"], None)
+    gx = along_lanes(0.5 * f["DF"] + 0.25 * f["DG"], 0.25 * f["DF"] + S6 * f["DG"], None)
+    odd = 0.5 * f["F"] + 0.25 * (f["G"] + f["EF"]) + S6 * f["EG"]
+    gy = pltpu.roll(odd, LANES - 1, 1) - pltpu.roll(odd, 1, 1)
+    return gz, gx, gy
+
+
+def conduct(own, other):
+    return 2.0 * own * other / jnp.maximum(own + other, 0.25)
+
+
+def choose(label, values):
+    out = jnp.zeros(label.shape, f32)
+    for k, v in enumerate(values):
+        out = jnp.where(label == float(k), v, out)
+    return out
+
+
+def solve_kernel(
+    where_ref, traits, intensity, temp, label, patch, got, far,
+    warm_out, v_out, mom_out,
+    cond, temp_a, temp_b, cap, power, gz, gx, gy, mod, expand, strain, prod, mats, inside, u, w,
+):
+    layers, rows, _ = temp.shape
+    full = far.shape[1]
+    half = layers // 2
+    me = where_ref[0]
+    pos = where_ref[2]
+    paired = where_ref[3] > 0
+    tiles = range(0, full, 8)
+    count = traits.shape[1]
+    sources = intensity.shape[0]
+    own = pl.multiple_of(me * rows, rows)
+    other = pl.multiple_of((1 - me) * rows, rows)
+    near_base = LANES // 2 - HALO * pos
+    far_base = (LANES - HALO) * (1 - pos)
+    lane_r = lane_of((rows, LANES))
+    near_lanes = (lane_r // HALO) == (near_base // HALO)
+    lane_f = lane_of((full, LANES))
+    far_lanes = (lane_f // HALO) == (far_base // HALO)
+
+    mean_mod = traits[2, 0]
+    for k in range(1, count):
+        mean_mod = mean_mod + traits[2, k]
+    scale = jnp.full((8, LANES), mean_mod * ((anchor_scale + 2.0 * CENTRE) / count), f32)
+    inv_scale = 1.0 / scale
+    cond_t = [traits[0, k] for k in range(count)]
+    cap_t = [time_step / jnp.full((8, LANES), traits[1, k], f32) for k in range(count)]
+    mod_t = [traits[2, k] for k in range(count)]
+    exp_t = [traits[3, k] for k in range(count)]
+    pow_t = [intensity[k] for k in range(sources)]
+
+    zero_tile = jnp.zeros((full + 2 * PAD, LANES), f32)
+    for ref in (cond, temp_a, temp_b, mod, strain, prod):
+        ref[0] = zero_tile
+        ref[layers + 1] = zero_tile
+    for ref in (u, w):
+        for b in range(ref.shape[0]):
+            for c in range(3):
+                ref[b, c, 0] = zero_tile
+                ref[b, c, layers + 1] = zero_tile
+    gz[0] = jnp.zeros((full, LANES), f32)
+    edge = jnp.zeros((PAD, LANES), f32)
+
+    def window(l, _):
+        for ref in (cond, temp_a, temp_b, mod, strain, prod, gx):
+            ref[l + 1, 0:PAD] = edge
+            ref[l + 1, PAD + full : 2 * PAD + full] = edge
+        for ref in (u, w):
+            for b in range(ref.shape[0]):
+                for c in range(3):
+                    ref[b, c, l + 1, 0:PAD] = edge
+                    ref[b, c, l + 1, PAD + full : 2 * PAD + full] = edge
+        for a, (ref, dest) in enumerate(((temp, temp_a), (label, temp_b), (patch, cond))):
+            mine = ref[l].astype(f32)
+            packed = got[a, lax.rem(l, half)]
+            theirs = jnp.where(l < half, packed, half_roll(packed))
+            near = pltpu.roll(got[a, half], (near_base - HALO * l + 2 * LANES) % LANES, 1)
+            theirs = jnp.where(near_lanes, near, theirs)
+            dest[l + 1, pl.ds(PAD + own, rows), :] = mine
+            dest[l + 1, pl.ds(PAD + other, rows), :] = theirs
+            edge_cols = pltpu.roll(far[a], (far_base - HALO * l + 2 * LANES) % LANES, 1)
+            if a == 1:
+                edge_cols = jnp.where(paired, edge_cols, -1.0)
+            old = dest[l + 1, PAD : PAD + full, :]
+            dest[l + 1, PAD : PAD + full, :] = jnp.where(far_lanes, edge_cols, old)
+        for r in tiles:
+            here = slice(PAD + r, PAD + r + 8)
+            there = slice(r, r + 8)
+            lab = temp_b[l + 1, here, :]
+            src = cond[l + 1, here, :]
+            cond[l + 1, here, :] = choose(lab, cond_t)
+            cap[l, there, :] = choose(lab, cap_t)
+            mod[l + 1, here, :] = choose(lab, mod_t)
+            expand[l, there, :] = choose(lab, exp_t)
+            power[l, there, :] = choose(src, pow_t)
+            if r == 0:
+                inside[...] = jnp.where(lab >= 0.0, 1.0, 0.0)
+        return 0
+
+    lax.fori_loop(0, layers, window, 0)
+
+    def faces(l, _):
+        for r in tiles:
+            here = slice(PAD + r, PAD + r + 8)
+            a = cond[l + 1, here, :]
+            gz[l + 1, r : r + 8, :] = conduct(a, cond[l + 2, here, :])
+            gx[l + 1, here, :] = conduct(a, cond[l + 1, PAD + r + 1 : PAD + r + 9, :])
+            gy[l, r : r + 8, :] = conduct(a, pltpu.roll(a, LANES - 1, 1))
+        return 0
+
+    lax.fori_loop(0, layers, faces, 0)
+
+    def heat(src, dst, last):
+        def step(l, _):
+            for r in tiles:
+                here = slice(PAD + r, PAD + r + 8)
+                there = slice(r, r + 8)
+                t = src[l + 1, here, :]
+                flux = gz[l + 1, there, :] * (src[l + 2, here, :] - t)
+                flux += gz[l, there, :] * (src[l, here, :] - t)
+                flux += gx[l + 1, here, :] * (src[l + 1, PAD + r + 1 : PAD + r + 9, :] - t)
+                flux += gx[l + 1, PAD + r - 1 : PAD + r + 7, :] * (
+                    src[l + 1, PAD + r - 1 : PAD + r + 7, :] - t
+                )
+                side = gy[l, there, :] * (pltpu.roll(t, LANES - 1, 1) - t)
+                flux += side - pltpu.roll(side, 1, 1)
+                new = t + cap[l, there, :] * (flux + power[l, there, :])
+                if last:
+                    warm_out[l, there, :] = new
+                    s = expand[l, there, :] * new
+                    strain[l + 1, here, :] = s
+                    prod[l + 1, here, :] = s * mod[l + 1, here, :]
+                else:
+                    dst[l + 1, here, :] = new
+            return 0
+
+        lax.fori_loop(0, layers, step, 0)
+
+    heat(temp_a, temp_b, False)
+    heat(temp_b, None, True)
+
+    mine8 = (lane_of((8, LANES)) // (LANES // 2)) == pos
+
+    def loads(l, acc):
+        for r in tiles:
+            here = slice(PAD + r, PAD + r + 8)
+            there = slice(r, r + 8)
+            s = picks(strain, None, l, r)
+            m = picks(mod, None, l, r)
+            q = picks(prod, None, l, r)
+            gs, gm, gq = gradient_stencil(s), gradient_stencil(m), gradient_stencil(q)
+            for k, entry in enumerate(matrix_stencil(m)):
+                mats[k, l, there, :] = entry * inv_scale
+            keep = inside[...]
+            for c in range(3):
+                v = (-0.5 * strain_gain) * (m["F"] * gs[c] + s["F"] * gm[c] + gq[c]) * keep
+                u[0, c, l + 1, here, :] = v
+                w[0, c, l + 1, here, :] = v * m["F"]
+                v_out[0, c, l, there, :] = v
+                acc = acc + jnp.where(mine8, v * v, 0.0)
+        return acc
+
+    zero = jnp.zeros((8, LANES), f32)
+    moments = [lax.fori_loop(0, layers, loads, zero)]
+
+    def power_step(number, src, dst):
+        def step(l, accs):
+            cross, square = accs
+            for r in tiles:
+                here = slice(PAD + r, PAD + r + 8)
+                there = slice(r, r + 8)
+                uz, ux, uy = (picks(u, (src, c), l, r) for c in range(3))
+                old = (uz["F"], ux["F"], uy["F"])
+                cu = full_stencil(uz, ux, uy)
+                wz, wx, wy = (picks(w, (src, c), l, r) for c in range(3))
+                weighted = (wz["F"], wx["F"], wy["F"])
+                cw = full_stencil(wz, wx, wy)
+                zz, xx, yy, zx, zy, xy = (mats[k, l, there, :] for k in range(6))
+                mixed = (
+                    zz * old[0] + zx * old[1] + zy * old[2],
+                    zx * old[0] + xx * old[1] + xy * old[2],
+                    zy * old[0] + xy * old[1] + yy * old[2],
+                )
+                m = mod[l + 1, here, :]
+                keep = inside[...]
+                for c in range(3):
+                    inner = (anchor_scale + CENTRE) * weighted[c] - m * cu[c] - cw[c]
+                    v = (inner * inv_scale + mixed[c] - old[c]) * keep
+                    v_out[number, c, l, there, :] = v
+                    if dst is not None:
+                        u[dst, c, l + 1, here, :] = v
+                        w[dst, c, l + 1, here, :] = v * m
+                    own_v = jnp.where(mine8, v, 0.0)
+                    cross = cross + own_v * old[c]
+                    square = square + own_v * own_v
+            return cross, square
+
+        return lax.fori_loop(0, layers, step, (zero, zero))
+
+    for number in range(1, ITERS + 1):
+        src = (number - 1) % 2
+        dst = number % 2 if number < ITERS else None
+        cross, square = power_step(number, src, dst)
+        moments.append(cross)
+        if number < ITERS:
+            moments.append(square)
+
+    lane1 = lane_of((1, LANES))
+    row = jnp.zeros((1, LANES), f32)
+    for k, part in enumerate(moments):
+        row = jnp.where(lane1 == k, jnp.sum(part), row)
+    for k in range(mom_out.shape[0]):
+        mom_out[k] = row
+
+
+def coefficients(mu, scale):
+    def inner(a, b):
+        total = None
+        for i, x in enumerate(a):
+            for j, y in enumerate(b):
+                term = x * y * mu[i + j]
+                total = term if total is None else total + term
+        return total
+
+    def added(a, b):
+        out = []
+        for k in range(max(len(a), len(b))):
+            if k >= len(a):
+                out.append(b[k])
+            elif k >= len(b):
+                out.append(a[k])
+            else:
+                out.append(a[k] + b[k])
+        return out
+
+    one = jnp.ones_like(mu[0])
+    residual = [one]
+    direction = [one]
+    solution = []
+    norm = mu[0]
+    for number in range(ITERS):
+        image = added(direction, [jnp.zeros_like(one)] + direction)
+        alpha = norm / inner(direction, image)
+        solution = added(solution, [alpha * d for d in direction])
+        residual = added(residual, [-alpha * d for d in image])
+        if number + 1 < ITERS:
+            following = inner(residual, residual)
+            ratio = following / norm
+            direction = added(residual, [ratio * d for d in direction])
+            norm = following
+    return [s / scale for s in solution], residual
+
+
+def combine_kernel(where_ref, traits, mom, v, warm, *outs):
+    layers, full, _ = warm.shape
+    rows = outs[0].shape[1]
+    half = layers // 2
+    quarter = half // 2
+    gx, gz, pos = where_ref[0], where_ref[1], where_ref[2]
+    total = jnp.sum(mom[:, 0, :], axis=0, keepdims=True)
+    lane1 = lane_of((1, LANES))
+    shape = (8, LANES)
+    mu = [
+        jnp.full(shape, jnp.sum(jnp.where(lane1 == k, total, 0.0)), f32) for k in range(2 * ITERS)
+    ]
+    count = traits.shape[1]
+    mean_mod = traits[2, 0]
+    for k in range(1, count):
+        mean_mod = mean_mod + traits[2, k]
+    scale = jnp.full(shape, mean_mod * ((anchor_scale + 2.0 * CENTRE) / count), f32)
+    sol, res = coefficients(mu, scale)
+    in_half = (lane_of(shape) // (LANES // 2)) == pos
+
+    for number, out in enumerate(outs):
+        dx, dz = number % 2, number // 2
+        row0 = pl.multiple_of((gx ^ dx) * rows, rows)
+        layer0 = (gz ^ dz) * half
+
+        def piece(l, _, out=out, row0=row0, layer0=layer0):
+            for r in range(0, rows, 8):
+                for c in range(3):
+                    made = []
+                    for ll in (l, l + quarter):
+                        vs = [v[k, c, layer0 + ll, pl.ds(row0 + r, 8), :] for k in range(ITERS + 1)]
+                        x = sol[0] * vs[0]
+                        y = res[0] * vs[0]
+                        for k in range(1, ITERS + 1):
+                            if k < ITERS:
+                                x = x + sol[k] * vs[k]
+                            y = y + res[k] * vs[k]
+                        made.append((x, y))
+                    for which in (0, 1):
+                        out[(3 * which + c) * quarter + l, r : r + 8, :] = jnp.where(
+                            in_half, made[0][which], half_roll(made[1][which])
+                        )
+            return 0
+
+        lax.fori_loop(0, quarter, piece, 0)
+        if dz == 0:
+            for l in range(half):
+                for r in range(0, rows, 8):
+                    low = warm[l, pl.ds(row0 + r, 8), :]
+                    high = warm[l + half, pl.ds(row0 + r, 8), :]
+                    out[6 * quarter + l, r : r + 8, :] = jnp.where(in_half, low, half_roll(high))
+
+
+def place_kernel(where_ref, mine, over_x, over_z, over_both, warm_out, sol_out, res_out):
+    layers, rows, _ = warm_out.shape
+    half = layers // 2
+    quarter = half // 2
+    gz, pos = where_ref[1], where_ref[2]
+    half_of = lane_of((rows, LANES)) // (LANES // 2)
+    for block, (a, b, p) in enumerate(((mine, over_x, pos), (over_z, over_both, 1 - pos))):
+        first = half_of == p
+        lanes = pl.ds(pl.multiple_of((gz ^ block) * LANES, LANES), LANES)
+        for which, out in enumerate((sol_out, res_out)):
+            for c in range(3):
+                for l in range(quarter):
+                    x = a[(3 * which + c) * quarter + l]
+                    y = b[(3 * which + c) * quarter + l]
+                    out[c, l, :, lanes] = jnp.where(first, x, y)
+                    out[c, l + quarter, :, lanes] = half_roll(jnp.where(first, y, x))
+        if block == 0:
+            for l in range(half):
+                x = a[6 * quarter + l]
+                y = b[6 * quarter + l]
+                warm_out[l] = jnp.where(first, x, y)
+                warm_out[l + half] = half_roll(jnp.where(first, y, x))
+
+
+def vmem():
+    return pl.BlockSpec(memory_space=pltpu.VMEM)
+
+
+def smem():
+    return pl.BlockSpec(memory_space=pltpu.SMEM)
+
+
+def per_device_fast(temp, label, patch, traits, intensity):
+    nx, ny, nz = (lax.axis_size(a) for a in AXES)
+    layers, rows, width = temp.shape
+    full = rows * nx
+    half = layers // 2
+    quarter = half // 2
+    devices = nx * ny * nz
+    gx, gy, gz = (lax.axis_index(a) for a in AXES)
+    pos = gx ^ gz
+    block = gy * nz + gz
+    paired = jnp.where(pos == 0, block > 0, block < ny * nz - 1)
+    where_am = jnp.stack([gx, gz, pos, paired.astype(jnp.int32)]).astype(jnp.int32)
+
+    def number(x, b):
+        return x * ny * nz + b
+
+    def everywhere(dx, dz):
+        return [
+            (number(x, y * nz + z), number(x ^ dx, y * nz + (z ^ dz)))
+            for x in range(nx) for y in range(ny) for z in range(nz)
+        ]
+
+    def side(x, b):
+        return x ^ (b % nz)
+
+    chain = []
+    for b in range(1, ny * nz):
+        left = [x for x in range(nx) if side(x, b - 1) == 1][0]
+        right = [x for x in range(nx) if side(x, b) == 0][0]
+        chain += [(number(left, b - 1), number(right, b)), (number(right, b), number(left, b - 1))]
+
+    sds = lambda *s: jax.ShapeDtypeStruct(s, f32)
+    send = pl.pallas_call(
+        pack_rows_kernel,
+        out_shape=sds(3, half + 1, rows, LANES),
+        in_specs=[smem(), vmem(), vmem(), vmem()],
+        out_specs=vmem(),
+        name="pack_rows",
+    )(where_am, temp, label, patch)
+    got = lax.ppermute(send, AXES, everywhere(1, 0))
+    send = pl.pallas_call(
+        pack_far_kernel,
+        out_shape=sds(3, full, LANES),
+        in_specs=[smem(), vmem(), vmem(), vmem(), vmem()],
+        out_specs=vmem(),
+        name="pack_far",
+    )(where_am, temp, label, patch, got)
+    far = lax.ppermute(send, AXES, chain)
+
+    padded = pltpu.VMEM((layers + 2, full + 2 * PAD, LANES), f32)
+    plain = pltpu.VMEM((layers, full, LANES), f32)
+    vectors = pltpu.VMEM((2, 3, layers + 2, full + 2 * PAD, LANES), f32)
+    warm, v, mom = pl.pallas_call(
+        solve_kernel,
+        out_shape=(
+            sds(layers, full, LANES),
+            sds(ITERS + 1, 3, layers, full, LANES),
+            sds(devices, 1, LANES),
+        ),
+        in_specs=[smem(), smem(), smem(), vmem(), vmem(), vmem(), vmem(), vmem()],
+        out_specs=(vmem(), vmem(), vmem()),
+        scratch_shapes=[
+            padded, padded, padded, plain, plain,
+            pltpu.VMEM((layers + 1, full, LANES), f32), padded, plain,
+            padded, plain, padded, padded,
+            pltpu.VMEM((6, layers, full, LANES), f32),
+            pltpu.VMEM((8, LANES), f32),
+            vectors, vectors,
+        ],
+        name="solve",
+    )(where_am, traits, intensity, temp, label, patch, got, far)
+    mom = lax.all_to_all(mom, AXES, 0, 0, tiled=True)
+    big = 6 * quarter + half
+    mine, to_x, to_z, to_both = pl.pallas_call(
+        combine_kernel,
+        out_shape=(
+            sds(big, rows, LANES), sds(big, rows, LANES),
+            sds(6 * quarter, rows, LANES), sds(6 * quarter, rows, LANES),
+        ),
+        in_specs=[smem(), smem(), vmem(), vmem(), vmem()],
+        out_specs=(vmem(),) * 4,
+        name="combine",
+    )(where_am, traits, mom, v, warm)
+    from_x = lax.ppermute(to_x, AXES, everywhere(1, 0))
+    from_z = lax.ppermute(to_z, AXES, everywhere(0, 1))
+    from_both = lax.ppermute(to_both, AXES, everywhere(1, 1))
+    return pl.pallas_call(
+        place_kernel,
+        out_shape=(
+            sds(layers, rows, width),
+            sds(3, half, rows, nz * width),
+            sds(3, half, rows, nz * width),
+        ),
+        in_specs=[smem(), vmem(), vmem(), vmem(), vmem()],
+        out_specs=(vmem(),) * 3,
+        name="place",
+    )(where_am, mine, from_x, from_z, from_both)
 
 
 def padded(value, sides, width):
@@ -29,10 +604,6 @@
     for number in range(count):
         summed = summed + jnp.where(identity == number, table[number], jnp.float32(0.0))
     return summed
-
-
-def conduct(own, other):
-    return 2.0 * own * other / jnp.maximum(own + other, 0.25)
 
 
 def heat_step(padded_temp, padded_cond, power, inverse_cap):
@@ -113,7 +684,7 @@
     return lax.psum((jnp.sum(residual * residual), jnp.sum(residual * image)), ("gx", "gy", "gz"))
 
 
-def per_device(
+def per_device_plain(
     starting_kelvin, substance_label, voxel_source_patch, substance_traits, patch_source_intensity
 ):
     count = substance_traits.shape[1]
@@ -178,6 +749,20 @@
         P(),
     )
     out_specs = (P(None, "gx", ("gy", "gz")), P(None, "gz", "gx", "gy"), P(None, "gz", "gx", "gy"))
+
+    def per_device(temp, label, patch, traits, intensity):
+        layers, rows, width = temp.shape
+        fits = (
+            mesh.shape["gx"] == 2
+            and mesh.shape["gz"] == 2
+            and width == LANES
+            and layers % 4 == 0
+            and layers * HALO <= LANES
+            and rows % 8 == 0
+        )
+        run = per_device_fast if fits else per_device_plain
+        return run(temp, label, patch, traits, intensity)
+
     return jax.shard_map(
         per_device, mesh=mesh, in_specs=in_specs, out_specs=out_specs, check_vma=False
     )

time: 373 us -> 78.2 us (0.21)
  blocking collectives: 120 us -> 19 us
  other arithmetic: 94.1 us -> 0.64 us
  waiting for transfers between devices: 72.8 us -> 14.4 us
  starting transfers between devices: 58.9 us -> 7.13 us
  Pallas kernels: 0 us -> 34.1 us
  local copies, waits for them, and re-layouts: 13.6 us -> 2.01 us
  between operations: 11.3 us -> 0.68 us
    psum x3 -> x0, blocking collectives: 120 us -> none  [two_products(): lax.psum((jnp.sum(residual * residual), jnp.sum(residual * image)), ('gx'...]
    another operation x12 -> x1, other arithmetic: 49.9 us -> 0.64 us  [per_device_fast(): jnp.stack([gx, gz, pos, paired.astype(jnp.int32)]).astype(jnp.int32)]
    ppermute x24 -> x5, waiting for transfers between devices: 63 us -> 14.4 us  [the longest x1 5.63 us: per_device_fast(): got = lax.ppermute(send, AXES, everywhere(1, 0))]
    ppermute x24 -> x5, starting transfers between devices: 55.3 us -> 7.13 us  [the longest x1 3 us: per_device_fast(): got = lax.ppermute(send, AXES, everywhere(1, 0))]
    pallas_call x0 -> x5, Pallas kernels: none -> 34.1 us  [the longest x1 23.4 us: per_device_fast(): pl.pallas_call(solve_kernel, out_shape=(sds(layers, full, LANES), sds(ITE...]
    all_to_all x0 -> x1, blocking collectives: none -> 19 us  [per_device_fast(): mom = lax.all_to_all(mom, AXES, 0, 0, tiled=True)]
    mul x1 -> x0, other arithmetic: 15.6 us -> none  [per_device(): strain = lookup(substance_label, substance_traits[3], count) * warmed_result]
    add x2 -> x0, other arithmetic: 13.2 us -> none  [the longest x1 13 us: heat_step(): return centre + time_step * inverse_cap * (heat_flux + power)]
  transfers between devices with their start and end apart: 25 -> 5, of which waited for: 21 -> 4; matrix products, arithmetic and copies ran while one was open for 1% -> 0% of each run, Pallas kernels for 0% -> 0%
where the time goes in v1:
time: 78.2 us; the launch traced here: 77.9 us
  Pallas kernels  34.1 us (44%)
  blocking collectives  19 us (24%)
  waiting for transfers between devices  14.4 us (18%)
  starting transfers between devices  7.13 us (9%)
  local copies, waits for them, and re-layouts  2.01 us (3%)
    pallas_call x1, Pallas kernels, per_device_fast(): pl.pallas_call(solve_kernel, out_shape=(sds(layers, full, LANES), sds(ITE...  23.4 us
    all_to_all x1, blocking collectives, per_device_fast(): mom = lax.all_to_all(mom, AXES, 0, 0, tiled=True)  19 us
    ppermute x1, waiting for transfers between devices, per_device_fast(): got = lax.ppermute(send, AXES, everywhere(1, 0))  5.63 us
    ppermute x1, waiting for transfers between devices, per_device_fast(): from_z = lax.ppermute(to_z, AXES, everywhere(0, 1))  5.05 us
    pallas_call x1, Pallas kernels, per_device_fast(): pl.pallas_call(combine_kernel, out_shape=(sds(big, rows, LANES), sds(big,...  4.47 us
    ppermute x1, waiting for transfers between devices, per_device_fast(): from_both = lax.ppermute(to_both, AXES, everywhere(1, 1))  3.61 us
    ppermute x1, starting transfers between devices, per_device_fast(): got = lax.ppermute(send, AXES, everywhere(1, 0))  3 us
    ppermute x1, starting transfers between devices, per_device_fast(): from_both = lax.ppermute(to_both, AXES, everywhere(1, 1))  2.41 us
  transfers between devices with their start and end apart: 5, of which 4 were waited for; matrix products, arithmetic and copies ran while one was open for 0% of the time, Pallas kernels for 0%

profile of v1, /device:TPU:0, one launch (start us, length us, event | category | flops | bytes accessed | tf_op | source)
XLA Modules:
  0.0 77.9 jit_solution(6496303326688697855)
XLA Ops:
  0.6 0.6 pad_add_fusion.where_ref
  1.3 2.0 %pack_rows.1 = f32[3,9,16,128]{3,2,1,0:T(8,128)} custom-call(s32[4]{0:T(128)} %pad_add_fusion.where_ref, f32[16,16,128]{2,1,0:T(8,128)} %temp.5, s32[16,16,128]{2,1,0:T(8,128)} %label.5, s32[16,16,128]{2,1,0:T(8,128)} %patch.5), custom_call_target="tpu_custom_call" | custom-call | tf_op jit(solution)/shard_map/pack_rows/pallas_call | solution.py:522
  3.2 3.0 %collective-permute-start = (f32[3,9,16,128]{3,2,1,0:T(8,128)}, f32[3,9,16,128]{3,2,1,0:T(8,128)S(1)}, u32[]{:S(2)}, u32[]{:S(2)}) collective-permute-start(f32[3,9,16,128]{3,2,1,0:T(8,128)} %pack_rows.1), channel_id=1, source_target_pairs={{0,16},{1,17},{2,18},{3,19},{4,20},{5,21},{6,22},{7,23},{8,24},{9,... | collective-permute-start | bytes 663560 | tf_op jit(solution)/shard_map/ppermute | solution.py:529
  6.2 5.6 %collective-permute-done.got = f32[3,9,16,128]{3,2,1,0:T(8,128)S(1)} collective-permute-done((f32[3,9,16,128]{3,2,1,0:T(8,128)}, f32[3,9,16,128]{3,2,1,0:T(8,128)S(1)}, u32[]{:S(2)}, u32[]{:S(2)}) %collective-permute-start) | collective-permute-done | bytes 221216 | tf_op jit(solution)/shard_map/ppermute | solution.py:529
  11.9 0.0 copy-start
  11.9 0.7 copy-done
  12.6 2.0 %pack_far.1 = f32[3,32,128]{2,1,0:T(8,128)} custom-call(s32[4]{0:T(128)} %pad_add_fusion.where_ref, f32[16,16,128]{2,1,0:T(8,128)} %temp.5, s32[16,16,128]{2,1,0:T(8,128)} %label.5, s32[16,16,128]{2,1,0:T(8,128)} %patch.5, f32[3,9,16,128]{3,2,1,0:T(8,128)} %copy-done), custom_call_target="tpu_custom_call" | custom-call | tf_op jit(solution)/shard_map/pack_far/pallas_call | solution.py:530
  14.6 0.7 collective-permute-start.1
  15.3 0.0 collective-permute-done.1.far
  15.3 0.0 copy-start.4
  15.3 0.6 copy-done.4
  15.9 23.4 %solve.1 = (f32[16,32,128]{2,1,0:T(8,128)}, f32[4,3,16,32,128]{4,3,2,1,0:T(8,128)}, f32[32,1,128]{2,1,0:T(1,128)}) custom-call(s32[4]{0:T(128)} %pad_add_fusion.where_ref, f32[4,4]{1,0:T(4,128)} %traits.3, f32[16]{0:T(128)} %intensity.1, f32[16,16,128]{2,1,0:T(8,128)} %temp.5, s32[16,16,128]{2,1,0:T(8,128)} %label.5, s32[16,16,128]{2,1,0:T(8,128)} %patch.5, ...), custom_call_target="tpu_custom_call" | custom-call | tf_op jit(solution)/shard_map/solve/pallas_call | solution.py:542
  39.3 19.0 %all_to_all.5.mom = f32[32,1,128]{2,1,0:T(1,128)} all-to-all(f32[32,1,128]{2,1,0:T(1,128)} %get-tuple-element.10), channel_id=1, replica_groups=mesh['gx'=2,'gy'=8,'gz'=2] {'gx','gy','gz'}, dimensions={0} | all-to-all | bytes 32768 | tf_op jit(solution)/shard_map/all_to_all | solution.py:561
  58.2 4.5 %combine.1 = (f32[32,16,128]{2,1,0:T(8,128)}, f32[32,16,128]{2,1,0:T(8,128)}, f32[24,16,128]{2,1,0:T(8,128)}, f32[24,16,128]{2,1,0:T(8,128)}) custom-call(s32[4]{0:T(128)} %pad_add_fusion.where_ref, f32[4,4]{1,0:T(4,128)} %traits.3, f32[32,1,128]{2,1,0:T(1,128)} %all_to_all.5.mom, f32[4,3,16,32,128]{4,3,2,1,0:T(8,128)} %get-tuple-element.11.v, ...), custom_call_target="tpu_custom_call" | custom-call | tf_op jit(solution)/shard_map/combine/pallas_call | solution.py:563
  62.7 0.6 collective-permute-start.2
  63.3 0.5 collective-permute-start.3
  63.8 2.4 %collective-permute-start.4 = (f32[24,16,128]{2,1,0:T(8,128)}, f32[24,16,128]{2,1,0:T(8,128)S(1)}, u32[]{:S(2)}, u32[]{:S(2)}) collective-permute-start(f32[24,16,128]{2,1,0:T(8,128)} %get-tuple-element.16), channel_id=1, source_target_pairs={{0,17},{1,16},{2,19},{3,18},{4,21},{5,20},{6,23},{7,22},{8,25},{9,... | collective-permute-start | bytes 589832 | tf_op jit(solution)/shard_map/ppermute | solution.py:575
  66.2 5.0 %collective-permute-done.3.over_z = f32[24,16,128]{2,1,0:T(8,128)S(1)} collective-permute-done((f32[24,16,128]{2,1,0:T(8,128)}, f32[24,16,128]{2,1,0:T(8,128)S(1)}, u32[]{:S(2)}, u32[]{:S(2)}) %collective-permute-start.3) | collective-permute-done | bytes 196640 | tf_op jit(solution)/shard_map/ppermute | solution.py:574
  71.3 3.6 %collective-permute-done.4.over_both = f32[24,16,128]{2,1,0:T(8,128)S(1)} collective-permute-done((f32[24,16,128]{2,1,0:T(8,128)}, f32[24,16,128]{2,1,0:T(8,128)S(1)}, u32[]{:S(2)}, u32[]{:S(2)}) %collective-permute-start.4) | collective-permute-done | bytes 196640 | tf_op jit(solution)/shard_map/ppermute | solution.py:575
  74.9 0.1 collective-permute-done.2.over_x
  75.0 0.0 copy-done.2
  75.0 0.5 copy-done.3
  75.5 0.2 copy-done.1
  75.7 2.2 %place.1 = (f32[16,16,128]{2,1,0:T(8,128)}, f32[3,8,16,256]{3,2,1,0:T(8,128)}, f32[3,8,16,256]{3,2,1,0:T(8,128)}) custom-call(s32[4]{0:T(128)} %pad_add_fusion.where_ref, f32[32,16,128]{2,1,0:T(8,128)} %get-tuple-element.13.mine, f32[32,16,128]{2,1,0:T(8,128)} %copy-done.1, f32[24,16,128]{2,1,0:T(8,128)} %copy-done.2, f32[24,16,128]{2,1,0:T(8,128)} %copy-done.3), custom_call_target="tpu_custom_call" | custom-call | tf_op jit(solution)/shard_map/place/pallas_call | solution.py:576
  (3 shorter events, 0.0 us)
Async XLA Ops:
  3.2 8.6 %collective-permute-start = (f32[3,9,16,128]{3,2,1,0:T(8,128)}, f32[3,9,16,128]{3,2,1,0:T(8,128)S(1)}, u32[]{:S(2)}, u32[]{:S(2)}) collective-permute-start(f32[3,9,16,128]{3,2,1,0:T(8,128)} %pack_rows.1), channel_id=1, source_target_pairs={{0,16},{1,17},{2,18},{3,19},{4,20},{5,21},{6,22},{7,23},{8,24},{9,... | collective-permute-start | bytes 663560 | tf_op jit(solution)/shard_map/ppermute | solution.py:529
  11.9 0.7 copy-start
  14.6 0.7 collective-permute-start.1
  15.3 0.6 copy-start.4
  62.7 12.3 %collective-permute-start.2 = (f32[32,16,128]{2,1,0:T(8,128)}, f32[32,16,128]{2,1,0:T(8,128)S(1)}, u32[]{:S(2)}, u32[]{:S(2)}) collective-permute-start(f32[32,16,128]{2,1,0:T(8,128)} %get-tuple-element.14), channel_id=1, source_target_pairs={{0,16},{1,17},{2,18},{3,19},{4,20},{5,21},{6,22},{7,23},{8,24},{9,... | collective-permute-start | bytes 786440 | tf_op jit(solution)/shard_map/ppermute | solution.py:573
  63.3 8.0 %collective-permute-start.3 = (f32[24,16,128]{2,1,0:T(8,128)}, f32[24,16,128]{2,1,0:T(8,128)S(1)}, u32[]{:S(2)}, u32[]{:S(2)}) collective-permute-start(f32[24,16,128]{2,1,0:T(8,128)} %get-tuple-element.15), channel_id=1, source_target_pairs={{0,1},{1,0},{2,3},{3,2},{4,5},{5,4},{6,7},{7,6},{8,9},{9,8},{10,11... | collective-permute-start | bytes 589832 | tf_op jit(solution)/shard_map/ppermute | solution.py:574
  63.8 11.1 %collective-permute-start.4 = (f32[24,16,128]{2,1,0:T(8,128)}, f32[24,16,128]{2,1,0:T(8,128)S(1)}, u32[]{:S(2)}, u32[]{:S(2)}) collective-permute-start(f32[24,16,128]{2,1,0:T(8,128)} %get-tuple-element.16), channel_id=1, source_target_pairs={{0,17},{1,16},{2,19},{3,18},{4,21},{5,20},{6,23},{7,22},{8,25},{9,... | collective-permute-start | bytes 589832 | tf_op jit(solution)/shard_map/ppermute | solution.py:575
  71.3 3.7 %copy-start.2 = (f32[24,16,128]{2,1,0:T(8,128)}, f32[24,16,128]{2,1,0:T(8,128)S(1)}, u32[]{:S(2)}) copy-start(f32[24,16,128]{2,1,0:T(8,128)S(1)} %collective-permute-done.3.over_z) | copy-start | bytes 589828
  74.9 0.7 copy-start.3
  75.0 0.7 copy-start.1

commit v2 on v1

--- a/solution.py
+++ b/solution.py
@@ -479,6 +479,13 @@
                 warm_out[l + half] = half_roll(jnp.where(first, y, x))
 
 
+LIMIT = 24 * 1024 * 1024
+
+
+def params():
+    return pltpu.CompilerParams(vmem_limit_bytes=LIMIT)
+
+
 def vmem():
     return pl.BlockSpec(memory_space=pltpu.VMEM)
 
@@ -519,22 +526,26 @@
         chain += [(number(left, b - 1), number(right, b)), (number(right, b), number(left, b - 1))]
 
     sds = lambda *s: jax.ShapeDtypeStruct(s, f32)
+    held = lambda *s: pltpu.VMEM(s, f32)
+    keep = lambda x: pltpu.with_memory_space_constraint(x, pltpu.VMEM)
     send = pl.pallas_call(
         pack_rows_kernel,
-        out_shape=sds(3, half + 1, rows, LANES),
+        out_shape=held(3, half + 1, rows, LANES),
         in_specs=[smem(), vmem(), vmem(), vmem()],
         out_specs=vmem(),
+        compiler_params=params(),
         name="pack_rows",
     )(where_am, temp, label, patch)
-    got = lax.ppermute(send, AXES, everywhere(1, 0))
+    got = keep(lax.ppermute(send, AXES, everywhere(1, 0)))
     send = pl.pallas_call(
         pack_far_kernel,
-        out_shape=sds(3, full, LANES),
+        out_shape=held(3, full, LANES),
         in_specs=[smem(), vmem(), vmem(), vmem(), vmem()],
         out_specs=vmem(),
+        compiler_params=params(),
         name="pack_far",
     )(where_am, temp, label, patch, got)
-    far = lax.ppermute(send, AXES, chain)
+    far = keep(lax.ppermute(send, AXES, chain))
 
     padded = pltpu.VMEM((layers + 2, full + 2 * PAD, LANES), f32)
     plain = pltpu.VMEM((layers, full, LANES), f32)
@@ -542,9 +553,9 @@
     warm, v, mom = pl.pallas_call(
         solve_kernel,
         out_shape=(
-            sds(layers, full, LANES),
-            sds(ITERS + 1, 3, layers, full, LANES),
-            sds(devices, 1, LANES),
+            held(layers, full, LANES),
+            held(ITERS + 1, 3, layers, full, LANES),
+            held(devices, 1, LANES),
         ),
         in_specs=[smem(), smem(), smem(), vmem(), vmem(), vmem(), vmem(), vmem()],
         out_specs=(vmem(), vmem(), vmem()),
@@ -556,23 +567,25 @@
             pltpu.VMEM((8, LANES), f32),
             vectors, vectors,
         ],
+        compiler_params=params(),
         name="solve",
     )(where_am, traits, intensity, temp, label, patch, got, far)
-    mom = lax.all_to_all(mom, AXES, 0, 0, tiled=True)
+    mom = keep(lax.all_to_all(mom, AXES, 0, 0, tiled=True))
     big = 6 * quarter + half
     mine, to_x, to_z, to_both = pl.pallas_call(
         combine_kernel,
         out_shape=(
-            sds(big, rows, LANES), sds(big, rows, LANES),
-            sds(6 * quarter, rows, LANES), sds(6 * quarter, rows, LANES),
+            held(big, rows, LANES), held(big, rows, LANES),
+            held(6 * quarter, rows, LANES), held(6 * quarter, rows, LANES),
         ),
         in_specs=[smem(), smem(), vmem(), vmem(), vmem()],
         out_specs=(vmem(),) * 4,
+        compiler_params=params(),
         name="combine",
-    )(where_am, traits, mom, v, warm)
-    from_x = lax.ppermute(to_x, AXES, everywhere(1, 0))
-    from_z = lax.ppermute(to_z, AXES, everywhere(0, 1))
-    from_both = lax.ppermute(to_both, AXES, everywhere(1, 1))
+    )(where_am, traits, mom, keep(v), keep(warm))
+    from_x = keep(lax.ppermute(to_x, AXES, everywhere(1, 0)))
+    from_z = keep(lax.ppermute(to_z, AXES, everywhere(0, 1)))
+    from_both = keep(lax.ppermute(to_both, AXES, everywhere(1, 1)))
     return pl.pallas_call(
         place_kernel,
         out_shape=(
@@ -582,8 +595,9 @@
         ),
         in_specs=[smem(), vmem(), vmem(), vmem(), vmem()],
         out_specs=(vmem(),) * 3,
+        compiler_params=params(),
         name="place",
-    )(where_am, mine, from_x, from_z, from_both)
+    )(where_am, keep(mine), from_x, from_z, from_both)
 
 
 def padded(value, sides, width):

time: 78.2 us -> 71.7 us (0.917)
  Pallas kernels: 34.1 us -> 26.8 us
  local copies, waits for them, and re-layouts: 2.01 us -> 4.04 us
    pallas_call x4, Pallas kernels: 31.8 us -> 25.1 us  [the longest x1 21.3 us: per_device_fast(): pl.pallas_call(solve_kernel, out_shape=(held(layers, full, LANES), held(I...]
    unnamed x10, local copies, waits for them, and re-layouts: 2.01 us -> 4.04 us
where the time goes in v2:
time: 71.7 us; the launch traced here: 71.5 us
  Pallas kernels  26.8 us (37%)
  blocking collectives  18.5 us (26%)
  waiting for transfers between devices  14.2 us (20%)
  starting transfers between devices  7.28 us (10%)
  local copies, waits for them, and re-layouts  4.04 us (6%)
    pallas_call x1, Pallas kernels, per_device_fast(): pl.pallas_call(solve_kernel, out_shape=(held(layers, full, LANES), held(I...  21.3 us
    all_to_all x1, blocking collectives, per_device_fast(): mom = keep(lax.all_to_all(mom, AXES, 0, 0, tiled=True))  18.5 us
    ppermute x1, waiting for transfers between devices, per_device_fast(): got = keep(lax.ppermute(send, AXES, everywhere(1, 0)))  5.43 us
    ppermute x1, waiting for transfers between devices, per_device_fast(): from_z = keep(lax.ppermute(to_z, AXES, everywhere(0, 1)))  4.82 us
    unnamed x10, local copies, waits for them, and re-layouts  4.04 us
    ppermute x1, waiting for transfers between devices, per_device_fast(): from_both = keep(lax.ppermute(to_both, AXES, everywhere(1, 1)))  3.79 us
    ppermute x1, starting transfers between devices, per_device_fast(): got = keep(lax.ppermute(send, AXES, everywhere(1, 0)))  3.06 us
    ppermute x1, starting transfers between devices, per_device_fast(): from_both = keep(lax.ppermute(to_both, AXES, everywhere(1, 1)))  2.38 us
  transfers between devices with their start and end apart: 5, of which 4 were waited for; matrix products, arithmetic and copies ran while one was open for 0% of the time, Pallas kernels for 0%

profile of v2, /device:TPU:0, one launch (start us, length us, event | category | flops | bytes accessed | tf_op | source)
XLA Modules:
  0.0 71.5 jit_solution(9809962998683462273)
XLA Ops:
  0.6 0.1 pad_add_fusion.where_ref
  0.7 0.0 copy-start
  0.7 0.9 %copy-done = f32[16,16,128]{2,1,0:T(8,128)S(1)} copy-done((f32[16,16,128]{2,1,0:T(8,128)S(1)}, f32[16,16,128]{2,1,0:T(8,128)}, u32[]{:S(2)}) %copy-start) | copy-done | bytes 131096
  1.6 0.9 %copy-done.1 = s32[16,16,128]{2,1,0:T(8,128)S(1)} copy-done((s32[16,16,128]{2,1,0:T(8,128)S(1)}, s32[16,16,128]{2,1,0:T(8,128)}, u32[]{:S(2)}) %copy-start.1) | copy-done | bytes 131096
  2.5 0.9 %copy-done.2 = s32[16,16,128]{2,1,0:T(8,128)S(1)} copy-done((s32[16,16,128]{2,1,0:T(8,128)S(1)}, s32[16,16,128]{2,1,0:T(8,128)}, u32[]{:S(2)}) %copy-start.2) | copy-done | bytes 131096
  3.4 0.8 %pack_rows.1 = f32[3,9,16,128]{3,2,1,0:T(8,128)S(1)} custom-call(s32[4]{0:T(128)S(1)} %pad_add_fusion.where_ref, f32[16,16,128]{2,1,0:T(8,128)S(1)} %copy-done, s32[16,16,128]{2,1,0:T(8,128)S(1)} %copy-done.1, s32[16,16,128]{2,1,0:T(8,128)S(1)} %copy-done.2), custom_call_target="tpu_custom_call" | custom-call | tf_op jit(solution)/shard_map/pack_rows/pallas_call | solution.py:531
  4.2 3.1 %collective-permute-start = (f32[3,9,16,128]{3,2,1,0:T(8,128)S(1)}, f32[3,9,16,128]{3,2,1,0:T(8,128)S(1)}, u32[]{:S(2)}, u32[]{:S(2)}) collective-permute-start(f32[3,9,16,128]{3,2,1,0:T(8,128)S(1)} %pack_rows.1), channel_id=1, source_target_pairs={{0,16},{1,17},{2,18},{3,19},{4,20},{5,21},{6,22},{7,23},{8,24},{9,... | collective-permute-start | bytes 663560 | tf_op jit(solution)/shard_map/ppermute | solution.py:539
  7.3 5.4 %collective-permute-done.got = f32[3,9,16,128]{3,2,1,0:T(8,128)S(1)} collective-permute-done((f32[3,9,16,128]{3,2,1,0:T(8,128)S(1)}, f32[3,9,16,128]{3,2,1,0:T(8,128)S(1)}, u32[]{:S(2)}, u32[]{:S(2)}) %collective-permute-start) | collective-permute-done | bytes 221216 | tf_op jit(solution)/shard_map/ppermute | solution.py:539
  12.7 0.8 %pack_far.1 = f32[3,32,128]{2,1,0:T(8,128)S(1)} custom-call(s32[4]{0:T(128)S(1)} %pad_add_fusion.where_ref, f32[16,16,128]{2,1,0:T(8,128)S(1)} %copy-done, s32[16,16,128]{2,1,0:T(8,128)S(1)} %copy-done.1, s32[16,16,128]{2,1,0:T(8,128)S(1)} %copy-done.2, f32[3,9,16,128]{3,2,1,0:T(8,128)S(1)} %collective-permute-done.got), custom_call_target="tpu_custom_call" | custom-call | tf_op jit(solution)/shard_map/pack_far/pallas_call | solution.py:540
  13.5 0.7 collective-permute-start.1
  14.2 0.0 collective-permute-done.1.far
  14.2 0.0 copy-start.3
  14.2 0.7 copy-done.3
  14.9 0.7 copy-done.4
  15.5 21.3 %solve.1 = (f32[16,32,128]{2,1,0:T(8,128)S(1)}, f32[4,3,16,32,128]{4,3,2,1,0:T(8,128)S(1)}, f32[32,1,128]{2,1,0:T(1,128)S(1)}) custom-call(s32[4]{0:T(128)S(1)} %pad_add_fusion.where_ref, f32[4,4]{1,0:T(4,128)S(1)} %copy-done.3, f32[16]{0:T(128)S(1)} %copy-done.4, f32[16,16,128]{2,1,0:T(8,128)S(1)} %copy-done, s32[16,16,128]{2,1,0:T(8,128)S(1)} %copy-done.1, ...), custom_call_target="tpu_custom_call" | custom-call | tf_op jit(solution)/shard_map/solve/pallas_call | solution.py:553
  36.8 18.5 %all_to_all.5.mom = f32[32,1,128]{2,1,0:T(1,128)S(1)} all-to-all(f32[32,1,128]{2,1,0:T(1,128)S(1)} %get-tuple-element.10), channel_id=1, replica_groups=mesh['gx'=2,'gy'=8,'gz'=2] {'gx','gy','gz'}, dimensions={0} | all-to-all | bytes 32768 | tf_op jit(solution)/shard_map/all_to_all | solution.py:573
  55.3 2.3 %combine.1 = (f32[32,16,128]{2,1,0:T(8,128)S(1)}, f32[32,16,128]{2,1,0:T(8,128)S(1)}, f32[24,16,128]{2,1,0:T(8,128)S(1)}, f32[24,16,128]{2,1,0:T(8,128)S(1)}) custom-call(s32[4]{0:T(128)S(1)} %pad_add_fusion.where_ref, f32[4,4]{1,0:T(4,128)S(1)} %copy-done.3, f32[32,1,128]{2,1,0:T(1,128)S(1)} %all_to_all.5.mom, ...), custom_call_target="tpu_custom_call" | custom-call | tf_op jit(solution)/shard_map/combine/pallas_call | solution.py:575
  57.6 0.6 collective-permute-start.2
  58.2 0.6 collective-permute-start.3
  58.8 2.4 %collective-permute-start.4 = (f32[24,16,128]{2,1,0:T(8,128)S(1)}, f32[24,16,128]{2,1,0:T(8,128)S(1)}, u32[]{:S(2)}, u32[]{:S(2)}) collective-permute-start(f32[24,16,128]{2,1,0:T(8,128)S(1)} %get-tuple-element.16), channel_id=1, source_target_pairs={{0,17},{1,16},{2,19},{3,18},{4,21},{5,20},{6,23},{7,22},{8,25},{9,... | collective-permute-start | bytes 589832 | tf_op jit(solution)/shard_map/ppermute | solution.py:588
  61.1 4.8 %collective-permute-done.3.over_z = f32[24,16,128]{2,1,0:T(8,128)S(1)} collective-permute-done((f32[24,16,128]{2,1,0:T(8,128)S(1)}, f32[24,16,128]{2,1,0:T(8,128)S(1)}, u32[]{:S(2)}, u32[]{:S(2)}) %collective-permute-start.3) | collective-permute-done | bytes 196640 | tf_op jit(solution)/shard_map/ppermute | solution.py:587
  66.0 3.8 %collective-permute-done.4.over_both = f32[24,16,128]{2,1,0:T(8,128)S(1)} collective-permute-done((f32[24,16,128]{2,1,0:T(8,128)S(1)}, f32[24,16,128]{2,1,0:T(8,128)S(1)}, u32[]{:S(2)}, u32[]{:S(2)}) %collective-permute-start.4) | collective-permute-done | bytes 196640 | tf_op jit(solution)/shard_map/ppermute | solution.py:588
  69.7 0.1 collective-permute-done.2.over_x
  69.9 1.6 %place.1 = (f32[16,16,128]{2,1,0:T(8,128)}, f32[3,8,16,256]{3,2,1,0:T(8,128)}, f32[3,8,16,256]{3,2,1,0:T(8,128)}) custom-call(s32[4]{0:T(128)S(1)} %pad_add_fusion.where_ref, f32[32,16,128]{2,1,0:T(8,128)S(1)} %get-tuple-element.13.mine, f32[32,16,128]{2,1,0:T(8,128)S(1)} %collective-permute-done.2.over_x, f32[24,16,128]{2,1,0:T(8,128)S(1)} %collective-permute-done.3.over_z, ...), custom_call_target="tpu_custom_call" | custom-call | tf_op jit(solution)/shard_map/place/pallas_call | solution.py:589
  (3 shorter events, 0.0 us)
Async XLA Ops:
  0.7 0.9 %copy-start = (f32[16,16,128]{2,1,0:T(8,128)S(1)}, f32[16,16,128]{2,1,0:T(8,128)}, u32[]{:S(2)}) copy-start(f32[16,16,128]{2,1,0:T(8,128)} %temp.5) | copy-start | bytes 393220
  1.6 0.9 %copy-start.1 = (s32[16,16,128]{2,1,0:T(8,128)S(1)}, s32[16,16,128]{2,1,0:T(8,128)}, u32[]{:S(2)}) copy-start(s32[16,16,128]{2,1,0:T(8,128)} %label.5) | copy-start | bytes 393220
  2.5 0.9 %copy-start.2 = (s32[16,16,128]{2,1,0:T(8,128)S(1)}, s32[16,16,128]{2,1,0:T(8,128)}, u32[]{:S(2)}) copy-start(s32[16,16,128]{2,1,0:T(8,128)} %patch.5) | copy-start | bytes 393220
  4.2 8.5 %collective-permute-start = (f32[3,9,16,128]{3,2,1,0:T(8,128)S(1)}, f32[3,9,16,128]{3,2,1,0:T(8,128)S(1)}, u32[]{:S(2)}, u32[]{:S(2)}) collective-permute-start(f32[3,9,16,128]{3,2,1,0:T(8,128)S(1)} %pack_rows.1), channel_id=1, source_target_pairs={{0,16},{1,17},{2,18},{3,19},{4,20},{5,21},{6,22},{7,23},{8,24},{9,... | collective-permute-start | bytes 663560 | tf_op jit(solution)/shard_map/ppermute | solution.py:539
  13.5 0.7 collective-permute-start.1
  14.2 0.7 copy-start.3
  14.9 0.7 copy-start.4
  57.6 12.3 %collective-permute-start.2 = (f32[32,16,128]{2,1,0:T(8,128)S(1)}, f32[32,16,128]{2,1,0:T(8,128)S(1)}, u32[]{:S(2)}, u32[]{:S(2)}) collective-permute-start(f32[32,16,128]{2,1,0:T(8,128)S(1)} %get-tuple-element.14), channel_id=1, source_target_pairs={{0,16},{1,17},{2,18},{3,19},{4,20},{5,21},{6,22},{7,23},{8,24},{9,... | collective-permute-start | bytes 786440 | tf_op jit(solution)/shard_map/ppermute | solution.py:586
  58.2 7.8 %collective-permute-start.3 = (f32[24,16,128]{2,1,0:T(8,128)S(1)}, f32[24,16,128]{2,1,0:T(8,128)S(1)}, u32[]{:S(2)}, u32[]{:S(2)}) collective-permute-start(f32[24,16,128]{2,1,0:T(8,128)S(1)} %get-tuple-element.15), channel_id=1, source_target_pairs={{0,1},{1,0},{2,3},{3,2},{4,5},{5,4},{6,7},{7,6},{8,9},{9,8},{10,11... | collective-permute-start | bytes 589832 | tf_op jit(solution)/shard_map/ppermute | solution.py:587
  58.8 11.0 %collective-permute-start.4 = (f32[24,16,128]{2,1,0:T(8,128)S(1)}, f32[24,16,128]{2,1,0:T(8,128)S(1)}, u32[]{:S(2)}, u32[]{:S(2)}) collective-permute-start(f32[24,16,128]{2,1,0:T(8,128)S(1)} %get-tuple-element.16), channel_id=1, source_target_pairs={{0,17},{1,16},{2,19},{3,18},{4,21},{5,20},{6,23},{7,22},{8,25},{9,... | collective-permute-start | bytes 589832 | tf_op jit(solution)/shard_map/ppermute | solution.py:588

commit v3 on v2

--- a/solution.py
+++ b/solution.py
@@ -7,8 +7,8 @@
 from jax.experimental.pallas import tpu as pltpu
 from jax.sharding import PartitionSpec as P
 
+
 ITERS = 3
-HEAT_STEPS = 2
 HALO = 8
 LANES = 128
 PAD = 8
@@ -30,27 +30,35 @@
     return lax.broadcasted_iota(jnp.int32, shape, 1)
 
 
-def pack_rows_kernel(where_ref, temp, label, patch, out):
+def pack_rows_kernel(where_ref, traits, intensity, temp, label, patch, block, out, table):
     layers, rows, _ = temp.shape
     half = layers // 2
     theirs = 1 - where_ref[2]
     lane = lane_of((rows, LANES))
     in_half = (lane // (LANES // 2)) == theirs
     base = LANES // 2 - HALO * theirs
+    kinds, count = traits.shape
+    for k in range(kinds):
+        for m in range(count):
+            table[k * count + m] = jnp.full((8, LANES), traits[k, m], f32)
+    for k in range(intensity.shape[0]):
+        table[kinds * count + k] = jnp.full((8, LANES), intensity[k], f32)
     for a, ref in enumerate((temp, label, patch)):
+        near = jnp.zeros((rows, LANES), f32)
+        values = []
+        for l in range(layers):
+            value = ref[l].astype(f32)
+            block[a, l] = value
+            values.append(value)
+            moved = pltpu.roll(value, (HALO * l - base) % LANES, 1)
+            near = jnp.where((lane // HALO) == l, moved, near)
         for l in range(half):
-            low = ref[l].astype(f32)
-            high = ref[l + half].astype(f32)
-            out[a, l] = jnp.where(in_half, low, half_roll(high))
-        near = jnp.zeros((rows, LANES), f32)
-        for l in range(layers):
-            moved = pltpu.roll(ref[l].astype(f32), (HALO * l - base) % LANES, 1)
-            near = jnp.where((lane // HALO) == l, moved, near)
+            out[a, l] = jnp.where(in_half, values[l], half_roll(values[l + half]))
         out[a, half] = near
 
 
-def pack_far_kernel(where_ref, temp, label, patch, got, out):
-    layers, rows, _ = temp.shape
+def pack_far_kernel(where_ref, block, got, out):
+    _, layers, rows, _ = block.shape
     half = layers // 2
     gx = where_ref[0]
     pos = where_ref[2]
@@ -58,12 +66,12 @@
     base = (LANES - HALO) * pos
     own = pl.multiple_of(gx * rows, rows)
     other = pl.multiple_of((1 - gx) * rows, rows)
-    for a, ref in enumerate((temp, label, patch)):
+    for a in range(3):
         mine = jnp.zeros((rows, LANES), f32)
         theirs = jnp.zeros((rows, LANES), f32)
         for l in range(layers):
             here = (lane // HALO) == l
-            moved = pltpu.roll(ref[l].astype(f32), (HALO * l - base) % LANES, 1)
+            moved = pltpu.roll(block[a, l], (HALO * l - base) % LANES, 1)
             mine = jnp.where(here, moved, mine)
             extra = 0 if l < half else LANES // 2
             moved = pltpu.roll(got[a, l % half], (HALO * l - base + extra) % LANES, 1)
@@ -76,7 +84,7 @@
     def at(dz, dx):
         if index is None:
             return ref[l + 1 + dz, PAD + row + dx : PAD + row + dx + 8, :]
-        return ref[index[0], index[1], l + 1 + dz, PAD + row + dx : PAD + row + dx + 8, :]
+        return ref[index, l + 1 + dz, PAD + row + dx : PAD + row + dx + 8, :]
 
     out = {}
     for dx in (-1, 0, 1):
@@ -166,49 +174,129 @@
     return out
 
 
-def solve_kernel(
-    where_ref, traits, intensity, temp, label, patch, got, far,
-    warm_out, v_out, mom_out,
-    cond, temp_a, temp_b, cap, power, gz, gx, gy, mod, expand, strain, prod, mats, inside, u, w,
+def shift_scale(table, count):
+    total = table[2 * count]
+    for k in range(1, count):
+        total = total + table[2 * count + k]
+    return total * ((anchor_scale + 2.0 * CENTRE) / count)
+
+
+def pack_vectors(where_ref, v, outs, warm):
+    count, _, layers, _, _ = v.shape
+    rows = outs[0].shape[1]
+    half = layers // 2
+    quarter = half // 2
+    gx, gz, pos = where_ref[0], where_ref[1], where_ref[2]
+    in_half = (lane_of((8, LANES)) // (LANES // 2)) == pos
+    for number, out in enumerate(outs):
+        dx, dz = number % 2, number // 2
+        row0 = pl.multiple_of((gx ^ dx) * rows, rows)
+        layer0 = (gz ^ dz) * half
+
+        def piece(l, _, out=out, row0=row0, layer0=layer0):
+            for r in range(0, rows, 8):
+                for k in range(count):
+                    for c in range(3):
+                        low = v[k, c, layer0 + l, pl.ds(row0 + r, 8), :]
+                        high = v[k, c, layer0 + l + quarter, pl.ds(row0 + r, 8), :]
+                        out[(3 * k + c) * quarter + l, r : r + 8, :] = jnp.where(
+                            in_half, low, half_roll(high)
+                        )
+            return 0
+
+        lax.fori_loop(0, quarter, piece, 0)
+        if warm is not None and dz == 0:
+
+            def warm_piece(l, _, out=out, row0=row0):
+                for r in range(0, rows, 8):
+                    low = warm[l, pl.ds(row0 + r, 8), :]
+                    high = warm[l + half, pl.ds(row0 + r, 8), :]
+                    out[3 * count * quarter + l, r : r + 8, :] = jnp.where(
+                        in_half, low, half_roll(high)
+                    )
+                return 0
+
+            lax.fori_loop(0, half, warm_piece, 0, unroll=2)
+
+
+def power_step(mod, mats, inside, inv_scale, mine8, source, dest, v):
+    u, w = source
+    layers = mats.shape[1]
+    tiles = range(0, mats.shape[2], 8)
+
+    def step(l, accs):
+        cross, square = accs
+        for r in tiles:
+            here = slice(PAD + r, PAD + r + 8)
+            there = slice(r, r + 8)
+            uz, ux, uy = (picks(u, c, l, r) for c in range(3))
+            old = (uz["F"], ux["F"], uy["F"])
+            cu = full_stencil(uz, ux, uy)
+            wz, wx, wy = (picks(w, c, l, r) for c in range(3))
+            weighted = (wz["F"], wx["F"], wy["F"])
+            cw = full_stencil(wz, wx, wy)
+            zz, xx, yy, zx, zy, xy = (mats[k, l, there, :] for k in range(6))
+            mixed = (
+                zz * old[0] + zx * old[1] + zy * old[2],
+                zx * old[0] + xx * old[1] + xy * old[2],
+                zy * old[0] + xy * old[1] + yy * old[2],
+            )
+            m = mod[l + 1, here, :]
+            keep = inside[...]
+            for c in range(3):
+                inner = (anchor_scale + CENTRE) * weighted[c] - m * cu[c] - cw[c]
+                new = (inner * inv_scale + mixed[c] - old[c]) * keep
+                v[c, l, there, :] = new
+                if dest is not None:
+                    dest[0][c, l + 1, here, :] = new
+                    dest[1][c, l + 1, here, :] = new * m
+                own = jnp.where(mine8, new, 0.0)
+                cross = cross + own * old[c]
+                square = square + own * own
+        return cross, square
+
+    zero = jnp.zeros((8, LANES), f32)
+    return lax.fori_loop(0, layers, step, (zero, zero))
+
+
+def clear_edges(refs, zero_tile):
+    for ref in refs:
+        for index in ([()] if len(ref.shape) == 3 else [(c,) for c in range(ref.shape[0])]):
+            ref[index + (0,)] = zero_tile
+            ref[index + (ref.shape[-3] - 1,)] = zero_tile
+
+
+def first_kernel(
+    where_ref, table, block, got, far,
+    mod, mats, inside, u_next, w_next, moments, mine, to_x, to_z, to_both,
+    cond, temp_a, temp_b, cap, power, gz, gx, gy, gy_back, expand, strain, prod, u, w, v, warm,
+    *, count,
 ):
-    layers, rows, _ = temp.shape
+    _, layers, rows, _ = block.shape
     full = far.shape[1]
     half = layers // 2
     me = where_ref[0]
     pos = where_ref[2]
     paired = where_ref[3] > 0
     tiles = range(0, full, 8)
-    count = traits.shape[1]
-    sources = intensity.shape[0]
+    kinds = 4
+    sources = table.shape[0] - kinds * count
     own = pl.multiple_of(me * rows, rows)
     other = pl.multiple_of((1 - me) * rows, rows)
     near_base = LANES // 2 - HALO * pos
     far_base = (LANES - HALO) * (1 - pos)
-    lane_r = lane_of((rows, LANES))
-    near_lanes = (lane_r // HALO) == (near_base // HALO)
-    lane_f = lane_of((full, LANES))
-    far_lanes = (lane_f // HALO) == (far_base // HALO)
-
-    mean_mod = traits[2, 0]
-    for k in range(1, count):
-        mean_mod = mean_mod + traits[2, k]
-    scale = jnp.full((8, LANES), mean_mod * ((anchor_scale + 2.0 * CENTRE) / count), f32)
-    inv_scale = 1.0 / scale
-    cond_t = [traits[0, k] for k in range(count)]
-    cap_t = [time_step / jnp.full((8, LANES), traits[1, k], f32) for k in range(count)]
-    mod_t = [traits[2, k] for k in range(count)]
-    exp_t = [traits[3, k] for k in range(count)]
-    pow_t = [intensity[k] for k in range(sources)]
+    near_lanes = (lane_of((rows, LANES)) // HALO) == (near_base // HALO)
+    far_lanes = (lane_of((full, LANES)) // HALO) == (far_base // HALO)
+
+    inv_scale = 1.0 / shift_scale(table, count)
+    cond_t = [table[k] for k in range(count)]
+    cap_t = [time_step / table[count + k] for k in range(count)]
+    mod_t = [table[2 * count + k] for k in range(count)]
+    exp_t = [table[3 * count + k] for k in range(count)]
+    pow_t = [table[kinds * count + k] for k in range(sources)]
 
     zero_tile = jnp.zeros((full + 2 * PAD, LANES), f32)
-    for ref in (cond, temp_a, temp_b, mod, strain, prod):
-        ref[0] = zero_tile
-        ref[layers + 1] = zero_tile
-    for ref in (u, w):
-        for b in range(ref.shape[0]):
-            for c in range(3):
-                ref[b, c, 0] = zero_tile
-                ref[b, c, layers + 1] = zero_tile
+    clear_edges((cond, temp_a, temp_b, mod, strain, prod, u, w, u_next, w_next), zero_tile)
     gz[0] = jnp.zeros((full, LANES), f32)
     edge = jnp.zeros((PAD, LANES), f32)
 
@@ -216,24 +304,27 @@
         for ref in (cond, temp_a, temp_b, mod, strain, prod, gx):
             ref[l + 1, 0:PAD] = edge
             ref[l + 1, PAD + full : 2 * PAD + full] = edge
-        for ref in (u, w):
-            for b in range(ref.shape[0]):
-                for c in range(3):
-                    ref[b, c, l + 1, 0:PAD] = edge
-                    ref[b, c, l + 1, PAD + full : 2 * PAD + full] = edge
-        for a, (ref, dest) in enumerate(((temp, temp_a), (label, temp_b), (patch, cond))):
-            mine = ref[l].astype(f32)
+        for ref in (u, w, u_next, w_next):
+            for c in range(3):
+                ref[c, l + 1, 0:PAD] = edge
+                ref[c, l + 1, PAD + full : 2 * PAD + full] = edge
+        for a, dest in enumerate((temp_a, temp_b, cond)):
             packed = got[a, lax.rem(l, half)]
             theirs = jnp.where(l < half, packed, half_roll(packed))
             near = pltpu.roll(got[a, half], (near_base - HALO * l + 2 * LANES) % LANES, 1)
             theirs = jnp.where(near_lanes, near, theirs)
-            dest[l + 1, pl.ds(PAD + own, rows), :] = mine
+            dest[l + 1, pl.ds(PAD + own, rows), :] = block[a, l]
             dest[l + 1, pl.ds(PAD + other, rows), :] = theirs
             edge_cols = pltpu.roll(far[a], (far_base - HALO * l + 2 * LANES) % LANES, 1)
             if a == 1:
                 edge_cols = jnp.where(paired, edge_cols, -1.0)
             old = dest[l + 1, PAD : PAD + full, :]
             dest[l + 1, PAD : PAD + full, :] = jnp.where(far_lanes, edge_cols, old)
+        return 0
+
+    lax.fori_loop(0, layers, window, 0, unroll=2)
+
+    def looked_up(l, _):
         for r in tiles:
             here = slice(PAD + r, PAD + r + 8)
             there = slice(r, r + 8)
@@ -248,18 +339,20 @@
                 inside[...] = jnp.where(lab >= 0.0, 1.0, 0.0)
         return 0
 
-    lax.fori_loop(0, layers, window, 0)
+    lax.fori_loop(0, layers, looked_up, 0)
 
     def faces(l, _):
         for r in tiles:
             here = slice(PAD + r, PAD + r + 8)
+            there = slice(r, r + 8)
             a = cond[l + 1, here, :]
-            gz[l + 1, r : r + 8, :] = conduct(a, cond[l + 2, here, :])
+            gz[l + 1, there, :] = conduct(a, cond[l + 2, here, :])
             gx[l + 1, here, :] = conduct(a, cond[l + 1, PAD + r + 1 : PAD + r + 9, :])
-            gy[l, r : r + 8, :] = conduct(a, pltpu.roll(a, LANES - 1, 1))
+            gy[l, there, :] = conduct(a, pltpu.roll(a, LANES - 1, 1))
+            gy_back[l, there, :] = conduct(a, pltpu.roll(a, 1, 1))
         return 0
 
-    lax.fori_loop(0, layers, faces, 0)
+    lax.fori_loop(0, layers, faces, 0, unroll=4)
 
     def heat(src, dst, last):
         def step(l, _):
@@ -273,11 +366,11 @@
                 flux += gx[l + 1, PAD + r - 1 : PAD + r + 7, :] * (
                     src[l + 1, PAD + r - 1 : PAD + r + 7, :] - t
                 )
-                side = gy[l, there, :] * (pltpu.roll(t, LANES - 1, 1) - t)
-                flux += side - pltpu.roll(side, 1, 1)
+                flux += gy[l, there, :] * (pltpu.roll(t, LANES - 1, 1) - t)
+                flux += gy_back[l, there, :] * (pltpu.roll(t, 1, 1) - t)
                 new = t + cap[l, there, :] * (flux + power[l, there, :])
                 if last:
-                    warm_out[l, there, :] = new
+                    warm[l, there, :] = new
                     s = expand[l, there, :] * new
                     strain[l + 1, here, :] = s
                     prod[l + 1, here, :] = s * mod[l + 1, here, :]
@@ -285,7 +378,7 @@
                     dst[l + 1, here, :] = new
             return 0
 
-        lax.fori_loop(0, layers, step, 0)
+        lax.fori_loop(0, layers, step, 0, unroll=4)
 
     heat(temp_a, temp_b, False)
     heat(temp_b, None, True)
@@ -304,64 +397,59 @@
                 mats[k, l, there, :] = entry * inv_scale
             keep = inside[...]
             for c in range(3):
-                v = (-0.5 * strain_gain) * (m["F"] * gs[c] + s["F"] * gm[c] + gq[c]) * keep
-                u[0, c, l + 1, here, :] = v
-                w[0, c, l + 1, here, :] = v * m["F"]
-                v_out[0, c, l, there, :] = v
-                acc = acc + jnp.where(mine8, v * v, 0.0)
+                new = (-0.5 * strain_gain) * (m["F"] * gs[c] + s["F"] * gm[c] + gq[c]) * keep
+                u[c, l + 1, here, :] = new
+                w[c, l + 1, here, :] = new * m["F"]
+                v[0, c, l, there, :] = new
+                acc = acc + jnp.where(mine8, new * new, 0.0)
         return acc
 
-    zero = jnp.zeros((8, LANES), f32)
-    moments = [lax.fori_loop(0, layers, loads, zero)]
-
-    def power_step(number, src, dst):
-        def step(l, accs):
-            cross, square = accs
-            for r in tiles:
-                here = slice(PAD + r, PAD + r + 8)
-                there = slice(r, r + 8)
-                uz, ux, uy = (picks(u, (src, c), l, r) for c in range(3))
-                old = (uz["F"], ux["F"], uy["F"])
-                cu = full_stencil(uz, ux, uy)
-                wz, wx, wy = (picks(w, (src, c), l, r) for c in range(3))
-                weighted = (wz["F"], wx["F"], wy["F"])
-                cw = full_stencil(wz, wx, wy)
-                zz, xx, yy, zx, zy, xy = (mats[k, l, there, :] for k in range(6))
-                mixed = (
-                    zz * old[0] + zx * old[1] + zy * old[2],
-                    zx * old[0] + xx * old[1] + xy * old[2],
-                    zy * old[0] + xy * old[1] + yy * old[2],
-                )
-                m = mod[l + 1, here, :]
-                keep = inside[...]
-                for c in range(3):
-                    inner = (anchor_scale + CENTRE) * weighted[c] - m * cu[c] - cw[c]
-                    v = (inner * inv_scale + mixed[c] - old[c]) * keep
-                    v_out[number, c, l, there, :] = v
-                    if dst is not None:
-                        u[dst, c, l + 1, here, :] = v
-                        w[dst, c, l + 1, here, :] = v * m
-                    own_v = jnp.where(mine8, v, 0.0)
-                    cross = cross + own_v * old[c]
-                    square = square + own_v * own_v
-            return cross, square
-
-        return lax.fori_loop(0, layers, step, (zero, zero))
-
-    for number in range(1, ITERS + 1):
-        src = (number - 1) % 2
-        dst = number % 2 if number < ITERS else None
-        cross, square = power_step(number, src, dst)
-        moments.append(cross)
-        if number < ITERS:
-            moments.append(square)
-
+    moments[0] = lax.fori_loop(0, layers, loads, jnp.zeros((8, LANES), f32))
+    cross, square = power_step(
+        mod, mats, inside, inv_scale, mine8, (u, w), (u_next, w_next), v.at[1]
+    )
+    moments[1] = cross
+    moments[2] = square
+    pack_vectors(where_ref, v, (mine, to_x, to_z, to_both), warm)
+
+
+def second_kernel(
+    where_ref, table, mod, mats, inside, u, w, moments,
+    mom_out, mine, to_x, to_z, to_both,
+    u_next, w_next, v,
+    *, count,
+):
+    layers = mats.shape[1]
+    full = mats.shape[2]
+    pos = where_ref[2]
+    inv_scale = 1.0 / shift_scale(table, count)
+    mine8 = (lane_of((8, LANES)) // (LANES // 2)) == pos
+    clear_edges((u_next, w_next), jnp.zeros((full + 2 * PAD, LANES), f32))
+    edge = jnp.zeros((PAD, LANES), f32)
+
+    def clear(l, _):
+        for ref in (u_next, w_next):
+            for c in range(3):
+                ref[c, l + 1, 0:PAD] = edge
+                ref[c, l + 1, PAD + full : 2 * PAD + full] = edge
+        return 0
+
+    lax.fori_loop(0, layers, clear, 0)
+    parts = [moments[k] for k in range(moments.shape[0])]
+    parts += power_step(
+        mod, mats, inside, inv_scale, mine8, (u, w), (u_next, w_next), v.at[0]
+    )
+    cross, _ = power_step(
+        mod, mats, inside, inv_scale, mine8, (u_next, w_next), None, v.at[1]
+    )
+    parts.append(cross)
     lane1 = lane_of((1, LANES))
     row = jnp.zeros((1, LANES), f32)
-    for k, part in enumerate(moments):
+    for k, part in enumerate(parts):
         row = jnp.where(lane1 == k, jnp.sum(part), row)
     for k in range(mom_out.shape[0]):
         mom_out[k] = row
+    pack_vectors(where_ref, v, (mine, to_x, to_z, to_both), None)
 
 
 def coefficients(mu, scale):
@@ -402,81 +490,56 @@
     return [s / scale for s in solution], residual
 
 
-def combine_kernel(where_ref, traits, mom, v, warm, *outs):
-    layers, full, _ = warm.shape
-    rows = outs[0].shape[1]
-    half = layers // 2
-    quarter = half // 2
-    gx, gz, pos = where_ref[0], where_ref[1], where_ref[2]
-    total = jnp.sum(mom[:, 0, :], axis=0, keepdims=True)
-    lane1 = lane_of((1, LANES))
-    shape = (8, LANES)
-    mu = [
-        jnp.full(shape, jnp.sum(jnp.where(lane1 == k, total, 0.0)), f32) for k in range(2 * ITERS)
-    ]
-    count = traits.shape[1]
-    mean_mod = traits[2, 0]
-    for k in range(1, count):
-        mean_mod = mean_mod + traits[2, k]
-    scale = jnp.full(shape, mean_mod * ((anchor_scale + 2.0 * CENTRE) / count), f32)
-    sol, res = coefficients(mu, scale)
-    in_half = (lane_of(shape) // (LANES // 2)) == pos
-
-    for number, out in enumerate(outs):
-        dx, dz = number % 2, number // 2
-        row0 = pl.multiple_of((gx ^ dx) * rows, rows)
-        layer0 = (gz ^ dz) * half
-
-        def piece(l, _, out=out, row0=row0, layer0=layer0):
-            for r in range(0, rows, 8):
-                for c in range(3):
-                    made = []
-                    for ll in (l, l + quarter):
-                        vs = [v[k, c, layer0 + ll, pl.ds(row0 + r, 8), :] for k in range(ITERS + 1)]
-                        x = sol[0] * vs[0]
-                        y = res[0] * vs[0]
-                        for k in range(1, ITERS + 1):
-                            if k < ITERS:
-                                x = x + sol[k] * vs[k]
-                            y = y + res[k] * vs[k]
-                        made.append((x, y))
-                    for which in (0, 1):
-                        out[(3 * which + c) * quarter + l, r : r + 8, :] = jnp.where(
-                            in_half, made[0][which], half_roll(made[1][which])
-                        )
-            return 0
-
-        lax.fori_loop(0, quarter, piece, 0)
-        if dz == 0:
-            for l in range(half):
-                for r in range(0, rows, 8):
-                    low = warm[l, pl.ds(row0 + r, 8), :]
-                    high = warm[l + half, pl.ds(row0 + r, 8), :]
-                    out[6 * quarter + l, r : r + 8, :] = jnp.where(in_half, low, half_roll(high))
-
-
-def place_kernel(where_ref, mine, over_x, over_z, over_both, warm_out, sol_out, res_out):
+def place_kernel(where_ref, table, mom, *refs, count):
+    early, late, outs = refs[:4], refs[4:8], refs[8:]
+    warm_out, sol_out, res_out = outs
     layers, rows, _ = warm_out.shape
     half = layers // 2
     quarter = half // 2
     gz, pos = where_ref[1], where_ref[2]
-    half_of = lane_of((rows, LANES)) // (LANES // 2)
-    for block, (a, b, p) in enumerate(((mine, over_x, pos), (over_z, over_both, 1 - pos))):
-        first = half_of == p
+    lane1 = lane_of((1, LANES))
+    shape = (8, LANES)
+    total = jnp.sum(mom[:, 0, :], axis=0, keepdims=True)
+    mu = [
+        jnp.full(shape, jnp.sum(jnp.where(lane1 == k, total, 0.0)), f32) for k in range(2 * ITERS)
+    ]
+    sol, res = coefficients(mu, shift_scale(table, count))
+    half_of = lane_of(shape) // (LANES // 2)
+    for block in range(2):
+        first = half_of == (pos if block == 0 else 1 - pos)
         lanes = pl.ds(pl.multiple_of((gz ^ block) * LANES, LANES), LANES)
-        for which, out in enumerate((sol_out, res_out)):
-            for c in range(3):
-                for l in range(quarter):
-                    x = a[(3 * which + c) * quarter + l]
-                    y = b[(3 * which + c) * quarter + l]
-                    out[c, l, :, lanes] = jnp.where(first, x, y)
-                    out[c, l + quarter, :, lanes] = half_roll(jnp.where(first, y, x))
+        a = (early[2 * block], late[2 * block])
+        b = (early[2 * block + 1], late[2 * block + 1])
+        for c in range(3):
+            for l in range(quarter):
+                for r in range(0, rows, 8):
+                    there = slice(r, r + 8)
+                    low, high = [], []
+                    for k in range(ITERS + 1):
+                        index = (3 * (k % 2) + c) * quarter + l
+                        x = a[k // 2][index, there, :]
+                        y = b[k // 2][index, there, :]
+                        low.append(jnp.where(first, x, y))
+                        high.append(jnp.where(first, y, x))
+                    for at, values in ((l, low), (l + quarter, high)):
+                        x = sol[0] * values[0]
+                        y = res[0] * values[0]
+                        for k in range(1, ITERS + 1):
+                            if k < ITERS:
+                                x = x + sol[k] * values[k]
+                            y = y + res[k] * values[k]
+                        if at != l:
+                            x, y = half_roll(x), half_roll(y)
+                        sol_out[c, at, there, lanes] = x
+                        res_out[c, at, there, lanes] = y
         if block == 0:
             for l in range(half):
-                x = a[6 * quarter + l]
-                y = b[6 * quarter + l]
-                warm_out[l] = jnp.where(first, x, y)
-                warm_out[l + half] = half_roll(jnp.where(first, y, x))
+                for r in range(0, rows, 8):
+                    there = slice(r, r + 8)
+                    x = a[0][6 * quarter + l, there, :]
+                    y = b[0][6 * quarter + l, there, :]
+                    warm_out[l, there, :] = jnp.where(first, x, y)
+                    warm_out[l + half, there, :] = half_roll(jnp.where(first, y, x))
 
 
 LIMIT = 24 * 1024 * 1024
@@ -528,76 +591,88 @@
     sds = lambda *s: jax.ShapeDtypeStruct(s, f32)
     held = lambda *s: pltpu.VMEM(s, f32)
     keep = lambda x: pltpu.with_memory_space_constraint(x, pltpu.VMEM)
-    send = pl.pallas_call(
+    there = lambda x: pltpu.with_memory_space_constraint(x, pltpu.HBM)
+    count = traits.shape[1]
+    entries = traits.size + intensity.size
+    own, send, table = pl.pallas_call(
         pack_rows_kernel,
-        out_shape=held(3, half + 1, rows, LANES),
-        in_specs=[smem(), vmem(), vmem(), vmem()],
-        out_specs=vmem(),
+        out_shape=(
+            held(3, layers, rows, LANES), held(3, half + 1, rows, LANES), held(entries, 8, LANES)
+        ),
+        in_specs=[smem(), smem(), smem(), vmem(), vmem(), vmem()],
+        out_specs=(vmem(),) * 3,
         compiler_params=params(),
         name="pack_rows",
-    )(where_am, temp, label, patch)
+    )(where_am, there(traits), there(intensity), there(temp), there(label), there(patch))
+    own, table = keep(own), keep(table)
     got = keep(lax.ppermute(send, AXES, everywhere(1, 0)))
     send = pl.pallas_call(
         pack_far_kernel,
         out_shape=held(3, full, LANES),
-        in_specs=[smem(), vmem(), vmem(), vmem(), vmem()],
+        in_specs=[smem(), vmem(), vmem()],
         out_specs=vmem(),
         compiler_params=params(),
         name="pack_far",
-    )(where_am, temp, label, patch, got)
+    )(where_am, own, got)
     far = keep(lax.ppermute(send, AXES, chain))
 
-    padded = pltpu.VMEM((layers + 2, full + 2 * PAD, LANES), f32)
-    plain = pltpu.VMEM((layers, full, LANES), f32)
-    vectors = pltpu.VMEM((2, 3, layers + 2, full + 2 * PAD, LANES), f32)
-    warm, v, mom = pl.pallas_call(
-        solve_kernel,
+    edged = (layers + 2, full + 2 * PAD, LANES)
+    plain = (layers, full, LANES)
+    padded = pltpu.VMEM(edged, f32)
+    flat = pltpu.VMEM(plain, f32)
+    vectors = pltpu.VMEM((3,) + edged, f32)
+    pieces = (6 * quarter + half, 6 * quarter + half, 6 * quarter, 6 * quarter)
+    first = pl.pallas_call(
+        functools.partial(first_kernel, count=count),
         out_shape=(
-            held(layers, full, LANES),
-            held(ITERS + 1, 3, layers, full, LANES),
-            held(devices, 1, LANES),
-        ),
-        in_specs=[smem(), smem(), smem(), vmem(), vmem(), vmem(), vmem(), vmem()],
-        out_specs=(vmem(), vmem(), vmem()),
+            held(*edged), held(6, *plain), held(8, LANES), held(3, *edged), held(3, *edged),
+            held(3, 8, LANES),
+        ) + tuple(held(k, rows, LANES) for k in pieces),
+        in_specs=[smem()] + [vmem()] * 4,
+        out_specs=(vmem(),) * 10,
         scratch_shapes=[
-            padded, padded, padded, plain, plain,
-            pltpu.VMEM((layers + 1, full, LANES), f32), padded, plain,
-            padded, plain, padded, padded,
-            pltpu.VMEM((6, layers, full, LANES), f32),
-            pltpu.VMEM((8, LANES), f32),
-            vectors, vectors,
+            padded, padded, padded, flat, flat,
+            pltpu.VMEM((layers + 1, full, LANES), f32), padded, flat, flat,
+            flat, padded, padded, vectors, vectors,
+            pltpu.VMEM((2, 3) + plain, f32), flat,
         ],
         compiler_params=params(),
-        name="solve",
-    )(where_am, traits, intensity, temp, label, patch, got, far)
-    mom = keep(lax.all_to_all(mom, AXES, 0, 0, tiled=True))
-    big = 6 * quarter + half
-    mine, to_x, to_z, to_both = pl.pallas_call(
-        combine_kernel,
-        out_shape=(
-            held(big, rows, LANES), held(big, rows, LANES),
-            held(6 * quarter, rows, LANES), held(6 * quarter, rows, LANES),
-        ),
-        in_specs=[smem(), smem(), vmem(), vmem(), vmem()],
-        out_specs=(vmem(),) * 4,
+        name="first",
+    )(where_am, table, own, got, far)
+    carried, early = first[:6], first[6:]
+
+    def exchanged(mine, *pieces):
+        moved = [mine]
+        for (dx, dz), piece in zip(((1, 0), (0, 1), (1, 1)), pieces):
+            moved.append(lax.ppermute(piece, AXES, everywhere(dx, dz)))
+        return tuple(keep(x) for x in moved)
+
+    early = exchanged(*early)
+    second = pl.pallas_call(
+        functools.partial(second_kernel, count=count),
+        out_shape=(held(devices, 1, LANES),)
+        + tuple(held(6 * quarter, rows, LANES) for _ in range(4)),
+        in_specs=[smem()] + [vmem()] * 7,
+        out_specs=(vmem(),) * 5,
+        scratch_shapes=[vectors, vectors, pltpu.VMEM((2, 3) + plain, f32)],
         compiler_params=params(),
-        name="combine",
-    )(where_am, traits, mom, keep(v), keep(warm))
-    from_x = keep(lax.ppermute(to_x, AXES, everywhere(1, 0)))
-    from_z = keep(lax.ppermute(to_z, AXES, everywhere(0, 1)))
-    from_both = keep(lax.ppermute(to_both, AXES, everywhere(1, 1)))
+        name="second",
+    )(where_am, table, *(keep(x) for x in carried))
+    late = exchanged(*second[1:])
+    mom = lax.all_to_all(second[0], AXES, 0, 0, tiled=True)
+    mom = keep(mom)
     return pl.pallas_call(
-        place_kernel,
+        functools.partial(place_kernel, count=count),
         out_shape=(
             sds(layers, rows, width),
             sds(3, half, rows, nz * width),
             sds(3, half, rows, nz * width),
         ),
-        in_specs=[smem(), vmem(), vmem(), vmem(), vmem()],
+        in_specs=[smem()] + [vmem()] * 10,
         out_specs=(vmem(),) * 3,
         compiler_params=params(),
         name="place",
-    )(where_am, keep(mine), from_x, from_z, from_both)
+    )(where_am, table, mom, *early, *late)
 
 
 def padded(value, sides, width):

time: 71.7 us -> 63 us (0.88)
  starting transfers between devices: 7.28 us -> 19 us
  blocking collectives: 18.5 us -> 11 us
  waiting for transfers between devices: 14.2 us -> 8.32 us
  local copies, waits for them, and re-layouts: 4.04 us -> 0 us
  Pallas kernels: 26.8 us -> 23.7 us
    ppermute x3 -> x6, starting transfers between devices: 3.55 us -> 15.2 us  [exchanged(): moved.append(lax.ppermute(piece, AXES, everywhere(dx, dz)))]
    all_to_all x1, blocking collectives: 18.5 us -> 11 us  [per_device_fast(): mom = lax.all_to_all(second[0], AXES, 0, 0, tiled=True)]
    ppermute x3 -> x6, waiting for transfers between devices: 8.73 us -> 2.89 us  [exchanged(): moved.append(lax.ppermute(piece, AXES, everywhere(dx, dz)))]
    unnamed x10 -> x0, local copies, waits for them, and re-layouts: 4.04 us -> none
    pallas_call x4, Pallas kernels: 25.9 us -> 22.9 us  [the longest x1 11.7 us: per_device_fast(): pl.pallas_call(functools.partial(first_kernel, count=count), out_shape=(h...]
  transfers between devices with their start and end apart: 5 -> 8, of which waited for: 4 -> 2; matrix products, arithmetic and copies ran while one was open for 0% -> 0% of each run, Pallas kernels for 0% -> 0%
where the time goes in v3:
time: 63 us; the launch traced here: 62.8 us
  Pallas kernels  23.7 us (38%)
  starting transfers between devices  19 us (30%)
  blocking collectives  11 us (17%)
  waiting for transfers between devices  8.32 us (13%)
  between operations  0.71 us (1%)
    ppermute x6, starting transfers between devices, exchanged(): moved.append(lax.ppermute(piece, AXES, everywhere(dx, dz)))  15.2 us
    pallas_call x1, Pallas kernels, per_device_fast(): pl.pallas_call(functools.partial(first_kernel, count=count), out_shape=(h...  11.7 us
    all_to_all x1, blocking collectives, per_device_fast(): mom = lax.all_to_all(second[0], AXES, 0, 0, tiled=True)  11 us
    pallas_call x1, Pallas kernels, per_device_fast(): pl.pallas_call(functools.partial(second_kernel, count=count), out_shape=(...  8 us
    ppermute x1, waiting for transfers between devices, per_device_fast(): got = keep(lax.ppermute(send, AXES, everywhere(1, 0)))  5.43 us
    ppermute x1, starting transfers between devices, per_device_fast(): got = keep(lax.ppermute(send, AXES, everywhere(1, 0)))  3.06 us
    ppermute x6, waiting for transfers between devices, exchanged(): moved.append(lax.ppermute(piece, AXES, everywhere(dx, dz)))  2.89 us
    pallas_call x1, Pallas kernels, per_device_fast(): pl.pallas_call(functools.partial(place_kernel, count=count), out_shape=(s...  1.91 us
  transfers between devices with their start and end apart: 8, of which 2 were waited for; matrix products, arithmetic and copies ran while one was open for 0% of the time, Pallas kernels for 0%

profile of v3, /device:TPU:0, one launch (start us, length us, event | category | flops | bytes accessed | tf_op | source)
XLA Modules:
  0.0 62.8 jit_solution(17527332557195538878)
XLA Ops:
  0.6 0.1 pad_add_fusion.where_ref
  0.7 1.3 %pack_rows.1 = (f32[3,16,16,128]{3,2,1,0:T(8,128)S(1)}, f32[3,9,16,128]{3,2,1,0:T(8,128)S(1)}, f32[32,8,128]{2,1,0:T(8,128)S(1)}) custom-call(s32[4]{0:T(128)S(1)} %pad_add_fusion.where_ref, f32[4,4]{1,0:T(4,128)} %traits.1, f32[16]{0:T(128)} %intensity.1, f32[16,16,128]{2,1,0:T(8,128)} %temp.1, s32[16,16,128]{2,1,0:T(8,128)} %label.1, s32[16,16,128]{2,1,0:T(8,128)} %patch.1), custom_call_target="tpu_custom_call" | custom-call | tf_op jit(solution)/shard_map/pack_rows/pallas_call | solution.py:597
  2.0 3.1 %collective-permute-start = (f32[3,9,16,128]{3,2,1,0:T(8,128)S(1)}, f32[3,9,16,128]{3,2,1,0:T(8,128)S(1)}, u32[]{:S(2)}, u32[]{:S(2)}) collective-permute-start(f32[3,9,16,128]{3,2,1,0:T(8,128)S(1)} %get-tuple-element.23), channel_id=1, source_target_pairs={{0,16},{1,17},{2,18},{3,19},{4,20},{5,21},{6,22},{7,23},{8,24},{9,... | collective-permute-start | bytes 663560 | tf_op jit(solution)/shard_map/ppermute | solution.py:608
  5.1 5.4 %collective-permute-done.got = f32[3,9,16,128]{3,2,1,0:T(8,128)S(1)} collective-permute-done((f32[3,9,16,128]{3,2,1,0:T(8,128)S(1)}, f32[3,9,16,128]{3,2,1,0:T(8,128)S(1)}, u32[]{:S(2)}, u32[]{:S(2)}) %collective-permute-start) | collective-permute-done | bytes 221216 | tf_op jit(solution)/shard_map/ppermute | solution.py:608
  10.5 0.8 %pack_far.1 = f32[3,32,128]{2,1,0:T(8,128)S(1)} custom-call(s32[4]{0:T(128)S(1)} %pad_add_fusion.where_ref, f32[3,16,16,128]{3,2,1,0:T(8,128)S(1)} %get-tuple-element.22.block, f32[3,9,16,128]{3,2,1,0:T(8,128)S(1)} %collective-permute-done.got), custom_call_target="tpu_custom_call" | custom-call | tf_op jit(solution)/shard_map/pack_far/pallas_call | solution.py:609
  11.3 0.7 %collective-permute-start.1 = (f32[3,32,128]{2,1,0:T(8,128)S(1)}, f32[3,32,128]{2,1,0:T(8,128)S(1)}, u32[]{:S(2)}, u32[]{:S(2)}) collective-permute-start(f32[3,32,128]{2,1,0:T(8,128)S(1)} %pack_far.1), channel_id=1, source_target_pairs={{16,17},{17,16},{1,2},{2,1},{18,19},{19,18},{3,4},{4,3},{20,21},{2... | collective-permute-start | bytes 147464 | tf_op jit(solution)/shard_map/ppermute | solution.py:617
  12.0 0.0 collective-permute-done.1.far
  12.0 11.7 %first.1 = (f32[18,48,128]{2,1,0:T(8,128)S(1)}, f32[6,16,32,128]{3,2,1,0:T(8,128)S(1)}, f32[8,128]{1,0:T(8,128)S(1)}, f32[3,18,48,128]{3,2,1,0:T(8,128)S(1)}, f3...) custom-call(s32[4]{0:T(128)S(1)} %pad_add_fusion.where_ref, ...), custom_call_target="tpu_custom_call" | custom-call | tf_op jit(solution)/shard_map/first/pallas_call | solution.py:625
  23.7 8.0 %second.1 = (f32[32,1,128]{2,1,0:T(1,128)S(1)}, f32[24,16,128]{2,1,0:T(8,128)S(1)}, f32[24,16,128]{2,1,0:T(8,128)S(1)}, f32[24,16,128]{2,1,0:T(8,128)S(1)}, f32[24,16,128]{2,1,0:T(8,128)S(1)}) custom-call(s32[4]{0:T(128)S(1)} %pad_add_fusion.where_ref, f32[32,8,128]{2,1,0:T(8,128)S(1)} %get-tuple-element.21.table, f32[18,48,128]{2,1,0:T(8,128)S(1)} %get-tuple-element.24.mod, ...), custom_call_target="tpu_custom_call" | custom-call | tf_op jit(solution)/shard_map/second/pallas_call | solution.py:651
  31.7 7.1 %collective-permute-start.5 = (f32[24,16,128]{2,1,0:T(8,128)S(1)}, f32[24,16,128]{2,1,0:T(8,128)S(1)}, u32[]{:S(2)}, u32[]{:S(2)}) collective-permute-start(f32[24,16,128]{2,1,0:T(8,128)S(1)} %get-tuple-element.36), channel_id=1, source_target_pairs={{0,16},{1,17},{2,18},{3,19},{4,20},{5,21},{6,22},{7,23},{8,24},{9,... | collective-permute-start | bytes 589832 | tf_op jit(solution)/shard_map/ppermute | solution.py:647
  38.8 0.1 collective-permute-start.2
  38.9 1.9 %collective-permute-start.6 = (f32[24,16,128]{2,1,0:T(8,128)S(1)}, f32[24,16,128]{2,1,0:T(8,128)S(1)}, u32[]{:S(2)}, u32[]{:S(2)}) collective-permute-start(f32[24,16,128]{2,1,0:T(8,128)S(1)} %get-tuple-element.37), channel_id=1, source_target_pairs={{0,1},{1,0},{2,3},{3,2},{4,5},{5,4},{6,7},{7,6},{8,9},{9,8},{10,11... | collective-permute-start | bytes 589832 | tf_op jit(solution)/shard_map/ppermute | solution.py:647
  40.8 1.6 %collective-permute-start.7 = (f32[24,16,128]{2,1,0:T(8,128)S(1)}, f32[24,16,128]{2,1,0:T(8,128)S(1)}, u32[]{:S(2)}, u32[]{:S(2)}) collective-permute-start(f32[24,16,128]{2,1,0:T(8,128)S(1)} %get-tuple-element.38), channel_id=1, source_target_pairs={{0,17},{1,16},{2,19},{3,18},{4,21},{5,20},{6,23},{7,22},{8,25},{9,... | collective-permute-start | bytes 589832 | tf_op jit(solution)/shard_map/ppermute | solution.py:647
  42.3 1.5 %collective-permute-start.3 = (f32[24,16,128]{2,1,0:T(8,128)S(1)}, f32[24,16,128]{2,1,0:T(8,128)S(1)}, u32[]{:S(2)}, u32[]{:S(2)}) collective-permute-start(f32[24,16,128]{2,1,0:T(8,128)S(1)} %get-tuple-element.33), channel_id=1, source_target_pairs={{0,1},{1,0},{2,3},{3,2},{4,5},{5,4},{6,7},{7,6},{8,9},{9,8},{10,11... | collective-permute-start | bytes 589832 | tf_op jit(solution)/shard_map/ppermute | solution.py:647
  43.8 2.9 %collective-permute-done.5.refs_5_ = f32[24,16,128]{2,1,0:T(8,128)S(1)} collective-permute-done((f32[24,16,128]{2,1,0:T(8,128)S(1)}, f32[24,16,128]{2,1,0:T(8,128)S(1)}, u32[]{:S(2)}, u32[]{:S(2)}) %collective-permute-start.5) | collective-permute-done | bytes 196640 | tf_op jit(solution)/shard_map/ppermute | solution.py:647
  46.7 3.1 %collective-permute-start.4 = (f32[24,16,128]{2,1,0:T(8,128)S(1)}, f32[24,16,128]{2,1,0:T(8,128)S(1)}, u32[]{:S(2)}, u32[]{:S(2)}) collective-permute-start(f32[24,16,128]{2,1,0:T(8,128)S(1)} %get-tuple-element.34), channel_id=1, source_target_pairs={{0,17},{1,16},{2,19},{3,18},{4,21},{5,20},{6,23},{7,22},{8,25},{9,... | collective-permute-start | bytes 589832 | tf_op jit(solution)/shard_map/ppermute | solution.py:647
  49.9 11.0 %all_to_all.5.mom = f32[32,1,128]{2,1,0:T(1,128)S(1)} all-to-all(f32[32,1,128]{2,1,0:T(1,128)S(1)} %get-tuple-element.30), channel_id=1, replica_groups=mesh['gx'=2,'gy'=8,'gz'=2] {'gx','gy','gz'}, dimensions={0} | all-to-all | bytes 32768 | tf_op jit(solution)/shard_map/all_to_all | solution.py:662
  60.9 0.0 collective-permute-done.6.refs_6_
  60.9 0.0 collective-permute-done.7.refs_7_
  60.9 0.0 collective-permute-done.3.refs_2_
  60.9 0.0 collective-permute-done.4.refs_3_
  60.9 0.0 collective-permute-done.2.refs_1_
  60.9 1.9 %place.1 = (f32[16,16,128]{2,1,0:T(8,128)}, f32[3,8,16,256]{3,2,1,0:T(8,128)}, f32[3,8,16,256]{3,2,1,0:T(8,128)}) custom-call(s32[4]{0:T(128)S(1)} %pad_add_fusion.where_ref, f32[32,8,128]{2,1,0:T(8,128)S(1)} %get-tuple-element.21.table, f32[32,1,128]{2,1,0:T(1,128)S(1)} %all_to_all.5.mom, f32[32,16,128]{2,1,0:T(8,128)S(1)} %get-tuple-element.31.refs_0_, ...), custom_call_target="tpu_custom_call" | custom-call | tf_op jit(solution)/shard_map/place/pallas_call | solution.py:664
Async XLA Ops:
  2.0 8.5 %collective-permute-start = (f32[3,9,16,128]{3,2,1,0:T(8,128)S(1)}, f32[3,9,16,128]{3,2,1,0:T(8,128)S(1)}, u32[]{:S(2)}, u32[]{:S(2)}) collective-permute-start(f32[3,9,16,128]{3,2,1,0:T(8,128)S(1)} %get-tuple-element.23), channel_id=1, source_target_pairs={{0,16},{1,17},{2,18},{3,19},{4,20},{5,21},{6,22},{7,23},{8,24},{9,... | collective-permute-start | bytes 663560 | tf_op jit(solution)/shard_map/ppermute | solution.py:608
  11.3 0.7 %collective-permute-start.1 = (f32[3,32,128]{2,1,0:T(8,128)S(1)}, f32[3,32,128]{2,1,0:T(8,128)S(1)}, u32[]{:S(2)}, u32[]{:S(2)}) collective-permute-start(f32[3,32,128]{2,1,0:T(8,128)S(1)} %pack_far.1), channel_id=1, source_target_pairs={{16,17},{17,16},{1,2},{2,1},{18,19},{19,18},{3,4},{4,3},{20,21},{2... | collective-permute-start | bytes 147464 | tf_op jit(solution)/shard_map/ppermute | solution.py:617
  31.7 15.0 %collective-permute-start.5 = (f32[24,16,128]{2,1,0:T(8,128)S(1)}, f32[24,16,128]{2,1,0:T(8,128)S(1)}, u32[]{:S(2)}, u32[]{:S(2)}) collective-permute-start(f32[24,16,128]{2,1,0:T(8,128)S(1)} %get-tuple-element.36), channel_id=1, source_target_pairs={{0,16},{1,17},{2,18},{3,19},{4,20},{5,21},{6,22},{7,23},{8,24},{9,... | collective-permute-start | bytes 589832 | tf_op jit(solution)/shard_map/ppermute | solution.py:647
  38.8 22.1 %collective-permute-start.2 = (f32[32,16,128]{2,1,0:T(8,128)S(1)}, f32[32,16,128]{2,1,0:T(8,128)S(1)}, u32[]{:S(2)}, u32[]{:S(2)}) collective-permute-start(f32[32,16,128]{2,1,0:T(8,128)S(1)} %get-tuple-element.32), channel_id=1, source_target_pairs={{0,16},{1,17},{2,18},{3,19},{4,20},{5,21},{6,22},{7,23},{8,24},{9,... | collective-permute-start | bytes 786440 | tf_op jit(solution)/shard_map/ppermute | solution.py:647
  38.9 21.9 %collective-permute-start.6 = (f32[24,16,128]{2,1,0:T(8,128)S(1)}, f32[24,16,128]{2,1,0:T(8,128)S(1)}, u32[]{:S(2)}, u32[]{:S(2)}) collective-permute-start(f32[24,16,128]{2,1,0:T(8,128)S(1)} %get-tuple-element.37), channel_id=1, source_target_pairs={{0,1},{1,0},{2,3},{3,2},{4,5},{5,4},{6,7},{7,6},{8,9},{9,8},{10,11... | collective-permute-start | bytes 589832 | tf_op jit(solution)/shard_map/ppermute | solution.py:647
  40.8 20.1 %collective-permute-start.7 = (f32[24,16,128]{2,1,0:T(8,128)S(1)}, f32[24,16,128]{2,1,0:T(8,128)S(1)}, u32[]{:S(2)}, u32[]{:S(2)}) collective-permute-start(f32[24,16,128]{2,1,0:T(8,128)S(1)} %get-tuple-element.38), channel_id=1, source_target_pairs={{0,17},{1,16},{2,19},{3,18},{4,21},{5,20},{6,23},{7,22},{8,25},{9,... | collective-permute-start | bytes 589832 | tf_op jit(solution)/shard_map/ppermute | solution.py:647
  42.3 18.5 %collective-permute-start.3 = (f32[24,16,128]{2,1,0:T(8,128)S(1)}, f32[24,16,128]{2,1,0:T(8,128)S(1)}, u32[]{:S(2)}, u32[]{:S(2)}) collective-permute-start(f32[24,16,128]{2,1,0:T(8,128)S(1)} %get-tuple-element.33), channel_id=1, source_target_pairs={{0,1},{1,0},{2,3},{3,2},{4,5},{5,4},{6,7},{7,6},{8,9},{9,8},{10,11... | collective-permute-start | bytes 589832 | tf_op jit(solution)/shard_map/ppermute | solution.py:647
  46.7 14.2 %collective-permute-start.4 = (f32[24,16,128]{2,1,0:T(8,128)S(1)}, f32[24,16,128]{2,1,0:T(8,128)S(1)}, u32[]{:S(2)}, u32[]{:S(2)}) collective-permute-start(f32[24,16,128]{2,1,0:T(8,128)S(1)} %get-tuple-element.34), channel_id=1, source_target_pairs={{0,17},{1,16},{2,19},{3,18},{4,21},{5,20},{6,23},{7,22},{8,25},{9,... | collective-permute-start | bytes 589832 | tf_op jit(solution)/shard_map/ppermute | solution.py:647
